TPU v7x, 32 devices: a whole 2x2x4 slice. The times are simulated.
32 devices in a mesh: dp: 8 (over y, x, core), vocab: 4 (over z).
Axes of the slice: x: 2, y: 2, z: 4, core: 2. Of those that a mesh axis runs over, the one named last changes fastest.
Arguments:
- resid: bfloat16 [2, 1024, 4096], P(None, 'dp'), may hold values from -6 to 6
- norm_gain: float32 [4096], replicated, may hold values from 0.5 to 1.5
- in_x: bfloat16 [4096, 4096], P('dp', 'vocab'), may hold values from -0.09375 to 0.09375
- in_z: bfloat16 [4096, 4096], P('dp', 'vocab'), may hold values from -0.09375 to 0.09375
- conv_w: float32 [4, 4096], P(None, 'vocab'), may hold values from -3 to 3
- conv_b: float32 [4096], P('vocab'), may hold values from -3 to 3
- xdt_w: bfloat16 [4096, 256], P('vocab'), may hold values from -0.09375 to 0.09375
- xbc_w: bfloat16 [4096, 32], P('vocab'), may hold values from -0.09375 to 0.09375
- dt_gain: float32 [256], replicated, may hold values from 0.5 to 1.5
- dt_proj: bfloat16 [256, 4096], P(None, 'vocab'), may hold values from -0.375 to 0.375
- dt_bias: float32 [4096], P('vocab'), may hold values from -4 to 1
- a_rate: float32 [4096, 16], P('vocab'), may hold values from 0.0001 to 1
- out_w: bfloat16 [4096, 4096], P('vocab'), may hold values from -0.09375 to 0.09375
- final_gain: float32 [4096], replicated, may hold values from 0.5 to 1.5
- head_w: bfloat16 [8192, 4096], P('vocab', 'dp'), as said below
- targets: int32 [2, 1024], P(None, 'dp'), may hold values from 0 to 8191
- lengths: int32 [2], replicated, may hold values from 256 to 1024
Outputs:
- hidden_out: bfloat16 [2, 1024, 4096], P(None, 'dp', 'vocab')
- token_logp: float32 [2, 1024], P(None, 'dp')
- mean_logp: float32 [], replicated
Inputs may be any that keep to these rules, and one draw needn't show every extreme that they name: `head_w`: entries lie within 720 / sqrt(4096) of zero.
All inputs are finite; a program needn't handle non-finite values.
Results may differ from a plain program's by a relative error of at most 0.019.
Values may be sent and summed in bfloat16 or wider, within the bound.
A program may use at most 128 MiB of HBM per device.

v0:
```python
import functools

import jax
import jax.numpy as jnp
from jax import lax
from jax.experimental import pallas as pl
from jax.experimental.pallas import tpu as pltpu
from jax.sharding import PartitionSpec as P

MESH = pl.DeviceIdType.MESH
VMEM = pl.BlockSpec(memory_space=pltpu.VMEM)
CHUNKS = 8
LANE = 128


def peer(axis, shift):
    size = lax.axis_size(axis)
    return {axis: lax.rem(lax.axis_index(axis) + shift, size)}


def greet(axes):
    barrier = pltpu.get_barrier_semaphore()
    count = 0
    for axis in axes:
        for shift in range(1, lax.axis_size(axis)):
            pl.semaphore_signal(barrier, inc=1, device_id=peer(axis, shift), device_id_type=MESH)
            count += 1
    pl.semaphore_wait(barrier, count)


def remote(src, dst, send_sem, recv_sem, device):
    return pltpu.make_async_remote_copy(
        src_ref=src, dst_ref=dst, send_sem=send_sem, recv_sem=recv_sem,
        device_id=device, device_id_type=MESH,
    )


def call(kernel, out_shape, scratch, cid, cost_us, name):
    return pl.pallas_call(
        kernel,
        out_shape=out_shape,
        scratch_shapes=scratch,
        compiler_params=pltpu.CompilerParams(
            collective_id=cid, has_side_effects=True, vmem_limit_bytes=56 * 1024 * 1024
        ),
        cost_estimate=pl.CostEstimate(
            flops=0, bytes_accessed=int(cost_us * 3.0e6), transcendentals=0
        ),
        name=name,
    )


def dt_kernel(nv, ranks, part_ref, gain_ref, out_ref, recv, mine, s1, r1, s2, r2):
    me = lax.axis_index("vocab")
    rows = part_ref.shape[0] // nv
    greet(("vocab",))
    copies = []
    for shift in range(1, nv):
        target = lax.rem(me + shift, nv)
        copy = remote(
            part_ref.at[pl.ds(pl.multiple_of(target * rows, rows), rows)], recv.at[shift - 1],
            s1.at[shift - 1], r1.at[shift - 1], peer("vocab", shift),
        )
        copy.start()
        copies.append(copy)
    own = pl.ds(pl.multiple_of(me * rows, rows), rows)
    total = part_ref[own, :].astype(jnp.float32)
    for shift in range(1, nv):
        copies[shift - 1].wait()
        total = total + recv[shift - 1].astype(jnp.float32)
    dt = total[:, :ranks]
    scale = lax.rsqrt(jnp.mean(dt * dt, axis=-1, keepdims=True) + 1e-06)
    mine[:, :ranks] = (dt * scale * gain_ref[...]).astype(jnp.bfloat16)
    mine[:, ranks:] = total[:, ranks:].astype(jnp.bfloat16)
    copies = []
    for shift in range(1, nv):
        copy = remote(
            mine, out_ref.at[own], s2.at[shift - 1], r2.at[shift - 1], peer("vocab", shift)
        )
        copy.start()
        copies.append(copy)
    out_ref[own, :] = mine[...]
    for copy in copies:
        copy.wait()


def dt_reduce(part, gain, nv, ranks):
    rows, cols = part.shape
    sems = [pltpu.SemaphoreType.DMA((nv - 1,))] * 4
    return call(
        functools.partial(dt_kernel, nv, ranks),
        jax.ShapeDtypeStruct((rows, cols), jnp.bfloat16),
        [
            pltpu.VMEM((nv - 1, rows // nv, cols), jnp.bfloat16),
            pltpu.VMEM((rows // nv, cols), jnp.bfloat16),
        ] + sems,
        1, 10, "dt_reduce",
    )(part, gain)


def scan_kernel(
    nd, batch, nstate, ranks, low_ref, proj_ref, bias_ref, conv_ref, rate_ref, out_ref,
    step, drive, maps, result, state, sums, agg, tot, agg_in, tot_in, s1, r1, s2, r2,
):
    me = lax.axis_index("dp")
    rows, chans = conv_ref.shape
    lanes = chans // LANE
    length = rows // batch
    span = length // CHUNKS
    greet(("dp",))
    low_dt = low_ref[:, :ranks]
    maps[...] = low_ref[:, ranks:].astype(jnp.float32)
    wide = 2 if lanes % 2 == 0 else 1
    size = wide * LANE

    @pl.loop(0, lanes // wide)
    def _(g):
        cols = pl.ds(pl.multiple_of(g * size, size), size)
        raw = jnp.dot(
            low_dt, proj_ref[:, cols], preferred_element_type=jnp.float32
        ) + bias_ref[:, cols]
        value = jnp.maximum(raw, 0.0) + jnp.log1p(jnp.exp(-jnp.abs(raw)))
        pushed = value * conv_ref[:, cols]
        for w in range(wide):
            k = g * wide + w
            step[k] = value[:, w * LANE : (w + 1) * LANE]
            drive[k] = pushed[:, w * LANE : (w + 1) * LANE]

    def run(with_out):
        @pl.loop(0, lanes // wide)
        def _(g):
            for b in range(batch):
                rates = [
                    [
                        rate_ref[pl.ds(n, 1), pl.ds(pl.multiple_of((g * wide + w) * LANE, LANE), LANE)]
                        for n in range(nstate)
                    ]
                    for w in range(wide)
                ]

                def one(t, carry):
                    at = pl.ds(b * length + t, CHUNKS, stride=span)
                    both = maps[at, :]
                    held, extra = carry
                    held, extra = list(held), list(extra)
                    now = [step[g * wide + w, at, :] for w in range(wide)]
                    push = [drive[g * wide + w, at, :] for w in range(wide)]
                    acc = [None] * wide
                    for n in range(nstate):
                        into = jnp.broadcast_to(both[:, n : n + 1], (CHUNKS, LANE))
                        if with_out:
                            outof = jnp.broadcast_to(
                                both[:, nstate + n : nstate + n + 1], (CHUNKS, LANE)
                            )
                        for w in range(wide):
                            i = w * nstate + n
                            held[i] = (
                                jnp.exp(-now[w] * rates[w][n]) * held[i] + push[w] * into
                            )
                            if with_out:
                                term = held[i] * outof
                                acc[w] = term if acc[w] is None else acc[w] + term
                    for w in range(wide):
                        if with_out:
                            result[g * wide + w, at, :] = acc[w]
                        else:
                            extra[w] = extra[w] + now[w]
                    return tuple(held), tuple(extra)

                zero = jnp.zeros((CHUNKS, LANE), jnp.float32)
                if with_out:
                    first = tuple(
                        state[b, g * wide + w, pl.ds(n * CHUNKS, CHUNKS), :]
                        for w in range(wide) for n in range(nstate)
                    )
                    lax.fori_loop(0, span, one, (first, ()))
                else:
                    held, extra = lax.fori_loop(
                        0, span, one, ((zero,) * (wide * nstate), (zero,) * wide)
                    )
                    for w in range(wide):
                        for n in range(nstate):
                            state[b, g * wide + w, pl.ds(n * CHUNKS, CHUNKS), :] = held[
                                w * nstate + n
                            ]
                        sums[b, g * wide + w] = extra[w]

    run(False)

    @pl.loop(0, lanes)
    def _(k):
        cols = pl.ds(pl.multiple_of(k * LANE, LANE), LANE)
        rate = rate_ref[:, cols]
        for b in range(batch):
            carry = jnp.zeros((nstate, LANE), jnp.float32)
            for c in range(CHUNKS):
                part = state[b, k, pl.ds(c, nstate, stride=CHUNKS), :]
                carry = jnp.exp(-sums[b, k, pl.ds(c, 1), :] * rate) * carry + part
            agg[pl.ds(b * nstate, nstate), cols] = carry.astype(jnp.bfloat16)
            tot[pl.ds(b, 1), cols] = jnp.sum(sums[b, k], axis=0, keepdims=True)

    def pair(source, target):
        device = {"dp": target}
        return (
            remote(agg, agg_in.at[source], s1.at[target], r1.at[source], device),
            remote(tot, tot_in.at[source], s2.at[target], r2.at[source], device),
        )

    for other in range(nd):
        @pl.when(other > me)
        def _():
            for copy in pair(me, other):
                copy.start()

    for other in range(nd):
        @pl.when(other < me)
        def _():
            for copy in pair(other, me):
                copy.wait_recv()

    @pl.loop(0, lanes)
    def _(k):
        cols = pl.ds(pl.multiple_of(k * LANE, LANE), LANE)
        rate = rate_ref[:, cols]
        for b in range(batch):
            def earlier(d, carry):
                decay = jnp.exp(-tot_in[d, pl.ds(b, 1), cols] * rate)
                return decay * carry + agg_in[d, pl.ds(b * nstate, nstate), cols].astype(
                    jnp.float32
                )

            carry = lax.fori_loop(0, me, earlier, jnp.zeros((nstate, LANE), jnp.float32))
            for c in range(CHUNKS):
                at = pl.ds(c, nstate, stride=CHUNKS)
                part = state[b, k, at, :]
                state[b, k, at, :] = carry
                carry = jnp.exp(-sums[b, k, pl.ds(c, 1), :] * rate) * carry + part

    run(True)

    @pl.loop(0, lanes)
    def _(k):
        out_ref[:, pl.ds(pl.multiple_of(k * LANE, LANE), LANE)] = result[k]

    for other in range(nd):
        @pl.when(other > me)
        def _():
            for copy in pair(me, other):
                copy.wait_send()


def scan(low, proj, bias, conv, rate, batch, nd, ranks):
    rows, chans = conv.shape
    nstate = rate.shape[0]
    lanes = chans // LANE
    big = pltpu.VMEM((lanes, rows, LANE), jnp.float32)
    return call(
        functools.partial(scan_kernel, nd, batch, nstate, ranks),
        jax.ShapeDtypeStruct((rows, chans), jnp.float32),
        [
            big, big,
            pltpu.VMEM((rows, low.shape[1] - ranks), jnp.float32),
            big,
            pltpu.VMEM((batch, lanes, nstate * CHUNKS, LANE), jnp.float32),
            pltpu.VMEM((batch, lanes, CHUNKS, LANE), jnp.float32),
            pltpu.VMEM((batch * nstate, chans), jnp.bfloat16),
            pltpu.VMEM((batch, chans), jnp.float32),
            pltpu.VMEM((nd, batch * nstate, chans), jnp.bfloat16),
            pltpu.VMEM((nd, batch, chans), jnp.float32),
        ] + [pltpu.SemaphoreType.DMA((nd,))] * 4,
        2, 30, "scan",
    )(low, proj, bias, conv, rate)


def out_kernel(nv, gated_ref, w_ref, resid_ref, out_ref, sent, recv, mine, s1, r1, s2, r2):
    me = lax.axis_index("vocab")
    rows, width = resid_ref.shape
    share = width // nv
    greet(("vocab",))

    def columns(index):
        return pl.ds(pl.multiple_of(index * share, share), share)

    tile = min(512, share)

    def product(index, put):
        @pl.loop(0, share // tile)
        def _(k):
            at = pl.multiple_of(index * share + k * tile, tile)
            put(
                pl.ds(pl.multiple_of(k * tile, tile), tile), pl.ds(at, tile),
                jnp.dot(
                    gated_ref[...], w_ref[:, pl.ds(at, tile)], preferred_element_type=jnp.float32
                ),
            )

    copies = {}
    order = sorted(range(1, nv), key=lambda s: abs(s - nv / 2))
    for shift in order:
        def put(local, whole, value):
            sent[shift - 1, :, local] = value.astype(jnp.bfloat16)

        product(lax.rem(me + shift, nv), put)
        copy = remote(
            sent.at[shift - 1], recv.at[shift - 1],
            s1.at[shift - 1], r1.at[shift - 1], peer("vocab", shift),
        )
        copy.start()
        copies[shift] = copy

    def put(local, whole, value):
        mine[:, local] = value

    product(me, put)
    for shift in order:
        copies[shift].wait()

    @pl.loop(0, share // tile)
    def _(k):
        local = pl.ds(pl.multiple_of(k * tile, tile), tile)
        whole = pl.ds(pl.multiple_of(me * share + k * tile, tile), tile)
        total = mine[:, local]
        for shift in range(1, nv):
            total = total + recv[shift - 1, :, local].astype(jnp.float32)
        hidden = (resid_ref[:, whole].astype(jnp.float32) + total).astype(jnp.bfloat16)
        sent[nv - 1, :, local] = hidden
        out_ref[:, whole] = hidden

    copies = []
    for shift in range(1, nv):
        copy = remote(
            sent.at[nv - 1], out_ref.at[:, columns(me)],
            s2.at[shift - 1], r2.at[shift - 1], peer("vocab", shift),
        )
        copy.start()
        copies.append(copy)
    for copy in copies:
        copy.wait()


def out_reduce(gated, w, resid, nv):
    rows, width = resid.shape
    share = width // nv
    sems = [pltpu.SemaphoreType.DMA((nv - 1,))] * 4
    return call(
        functools.partial(out_kernel, nv),
        jax.ShapeDtypeStruct((rows, width), jnp.bfloat16),
        [
            pltpu.VMEM((nv, rows, share), jnp.bfloat16),
            pltpu.VMEM((nv - 1, rows, share), jnp.bfloat16),
            pltpu.VMEM((rows, share), jnp.float32),
        ] + sems,
        3, 60, "out_reduce",
    )(gated, w, resid)


def tail_kernel(nv, nd, stats_ref, mask_ref, logp_ref, sum_ref, recv, part, parts, s1, r1, s2, r2):
    greet(("vocab", "dp"))
    copies = []
    for shift in range(1, nv):
        copy = remote(
            stats_ref, recv.at[shift - 1], s1.at[shift - 1], r1.at[shift - 1],
            peer("vocab", shift),
        )
        copy.start()
        copies.append(copy)
    for copy in copies:
        copy.wait()
    everyone = [stats_ref[...]] + [recv[k] for k in range(nv - 1)]
    top = everyone[0][0:1]
    for stats in everyone[1:]:
        top = jnp.maximum(top, stats[0:1])
    total = jnp.zeros_like(top)
    picked = jnp.zeros_like(top)
    for stats in everyone:
        total = total + stats[1:2] * jnp.exp(stats[0:1] - top)
        picked = picked + stats[2:3]
    logp = picked - (top + jnp.log(total))
    logp_ref[...] = logp
    masked = jnp.sum(jnp.where(mask_ref[...] > 0.0, logp, 0.0), axis=-1, keepdims=True)
    part[...] = jnp.broadcast_to(masked, part.shape)
    copies = []
    for shift in range(1, nd):
        copy = remote(
            part, parts.at[shift - 1], s2.at[shift - 1], r2.at[shift - 1], peer("dp", shift)
        )
        copy.start()
        copies.append(copy)
    grand = part[...]
    for shift in range(1, nd):
        copies[shift - 1].wait()
        grand = grand + parts[shift - 1]
    sum_ref[...] = grand


def tail(stats, mask, nv, nd):
    rows = stats.shape[1]
    return call(
        functools.partial(tail_kernel, nv, nd),
        (
            jax.ShapeDtypeStruct((1, rows), jnp.float32),
            jax.ShapeDtypeStruct((8, 128), jnp.float32),
        ),
        [
            pltpu.VMEM((nv - 1, 8, rows), jnp.float32),
            pltpu.VMEM((8, 128), jnp.float32),
            pltpu.VMEM((nd - 1, 8, 128), jnp.float32),
        ] + [pltpu.SemaphoreType.DMA((nv - 1,))] * 2 + [pltpu.SemaphoreType.DMA((nd - 1,))] * 2,
        4, 6, "tail",
    )(stats, mask)


def rms_norm(values, gain, epsilon):
    return values * lax.rsqrt(jnp.mean(values * values, axis=-1, keepdims=True) + epsilon) * gain


def body(
    resid, norm_gain, in_x, in_z, conv_w, conv_b, xdt_w, xbc_w, dt_gain, dt_proj, dt_bias,
    a_rate, out_w, final_gain, head_w, targets, lengths,
):
    nv, nd = lax.axis_size("vocab"), lax.axis_size("dp")
    batch, local_len, width = resid.shape
    channels = in_x.shape[1]
    nstate = a_rate.shape[1]
    ranks = xdt_w.shape[1]
    kernel_len = conv_w.shape[0]
    rows = batch * local_len
    vocab_index = lax.axis_index("vocab")

    full_x = lax.all_gather(in_x, "dp", axis=0, tiled=True)
    in_z, _ = lax.optimization_barrier((in_z, in_x))
    full_z = lax.all_gather(in_z, "dp", axis=0, tiled=True)
    full_head = lax.all_gather(head_w, "dp", axis=1, tiled=True)

    pad = -(2 * nstate) % 128
    low_w = jnp.concatenate([xdt_w, xbc_w, jnp.zeros((channels, pad), jnp.bfloat16)], axis=1)
    flat = resid.reshape(rows, width)
    stream = flat.astype(jnp.float32)
    normed = rms_norm(stream, norm_gain, 1e-05).astype(jnp.bfloat16)
    x_inner = (
        jnp.dot(normed, full_x, preferred_element_type=jnp.float32)
        .astype(jnp.bfloat16)
        .reshape(batch, local_len, channels)
    )
    before = lax.ppermute(
        x_inner[:, local_len - (kernel_len - 1) :, :], "dp", [(i, i + 1) for i in range(nd - 1)]
    )
    padded = jnp.concatenate([before, x_inner], axis=1).astype(jnp.float32)
    conv_sum = jnp.zeros((batch, local_len, channels), jnp.float32) + conv_b
    for tap in range(kernel_len):
        conv_sum = conv_sum + conv_w[tap] * padded[:, tap : tap + local_len, :]
    conv_act = jax.nn.silu(conv_sum).reshape(rows, channels)
    part = jnp.dot(
        conv_act.astype(jnp.bfloat16), low_w, preferred_element_type=jnp.float32
    ).astype(jnp.bfloat16)
    low = dt_reduce(part, dt_gain[None, :], nv, ranks)
    mixed = scan(low, dt_proj, dt_bias[None, :], conv_act, a_rate.T, batch, nd, ranks)
    z_gate = (
        jnp.dot(normed, full_z, preferred_element_type=jnp.float32)
        .astype(jnp.bfloat16)
        .astype(jnp.float32)
    )
    gated = (mixed * jax.nn.silu(z_gate)).astype(jnp.bfloat16)
    hidden = out_reduce(gated, out_w, flat, nv)
    share = width // nv
    hidden_share = lax.dynamic_slice_in_dim(hidden, vocab_index * share, share, 1)
    final = rms_norm(hidden.astype(jnp.float32), final_gain, 1e-05).astype(jnp.bfloat16)
    logits = lax.dot_general(
        final, full_head, (((1,), (1,)), ((), ())), preferred_element_type=jnp.float32
    )
    vocab_rows = head_w.shape[0]
    local_ids = targets.reshape(rows) - vocab_index * vocab_rows
    entry_ids = lax.broadcasted_iota(jnp.int32, (rows, vocab_rows), 1)
    picked = jnp.sum(jnp.where(entry_ids == local_ids[:, None], logits, 0.0), axis=-1)
    top = jnp.max(logits, axis=-1)
    total = jnp.sum(jnp.exp(logits - top[:, None]), axis=-1)
    stats = jnp.concatenate(
        [top[None], total[None], picked[None], jnp.zeros((5, rows), jnp.float32)], axis=0
    )
    positions = lax.axis_index("dp") * local_len + jnp.arange(local_len, dtype=jnp.int32)
    mask = (positions[None, :] < lengths[:, None]).astype(jnp.float32).reshape(1, rows)
    logp, grand = tail(stats, mask, nv, nd)
    mean_logp = grand[0, 0] / jnp.sum(lengths.astype(jnp.float32))
    return (
        hidden_share.reshape(batch, local_len, share),
        logp.reshape(batch, local_len),
        mean_logp,
    )


def solution(mesh):
    in_specs = (
        P(None, "dp", None), P(), P("dp", "vocab"), P("dp", "vocab"), P(None, "vocab"), P("vocab"),
        P("vocab", None), P("vocab", None), P(), P(None, "vocab"), P("vocab"), P("vocab", None),
        P("vocab", None), P(), P("vocab", "dp"), P(None, "dp"), P(),
    )
    out_specs = (P(None, "dp", "vocab"), P(None, "dp"), P())
    return jax.shard_map(body, mesh=mesh, in_specs=in_specs, out_specs=out_specs, check_vma=False)
```

profile of v0, /device:TPU:0, one launch (start us, length us, event | category | flops | bytes accessed | tf_op | source)
XLA Modules:
  0.0 293.9 jit_solution(10398252869500459722)
XLA Ops:
  7.2 0.0 copy-start.1
  7.2 0.0 all-gather.4.cloned.1.call-start
  7.2 0.7 all-gather.4.cloned.1.call-update
  7.9 0.0 all-gather.6.cloned.1.call-start
  8.0 0.7 all-gather.6.cloned.1.call-update
  8.7 0.0 copy-start.6
  8.7 0.0 copy-start.7
  8.7 0.0 copy-start.4
  8.7 0.0 copy-start.9
  8.7 0.0 all-gather.8.cloned.1.call-start
  8.7 0.7 all-gather.8.cloned.1.call-update
  9.5 0.0 copy-done.1
  9.5 0.5 multiply_reduce_fusion
  10.0 0.0 copy-done.6
  10.0 0.0 copy-done.7
  10.0 0.6 compare_convert_fusion
  10.6 0.0 copy-done.4
  10.7 56.2 %all-gather.4.cloned.1.call-done = bf16[4096,1024]{1,0:T(8,128)(2,1)} async-done(((bf16[512,1024]{1,0:T(8,128)(2,1)}), bf16[4096,1024]{1,0:T(8,128)(2,1)}) %all-gather.4.cloned.1.call-update) | async-done | bytes 8388624 | tf_op jit(solution)/shard_map/all_gather | solution.py:430
  66.9 0.0 copy-done.9
  66.9 5.8 %convolution_convert_fusion.1 = bf16[256,1024]{1,0:T(8,128)(2,1)S(1)} fusion(bf16[4096,1024]{1,0:T(8,128)(2,1)} %all-gather.4.cloned.1.call-done, bf16[256,4096]{1,0:T(8,128)(2,1)S(1)} %bitcast.25, f32[4096]{0:T(1024)S(1)} %copy-done.9, f32[256]{0:T(256)S(1)} %rsqrt_bitcast_fusion), kind=kOutput, calls=%fused_computation.16 | convolution fusion | flops 2151940096 | bytes 11027456 | tf_op jit(solution)/shard_map/dot_general | solution.py:441
  72.7 2.3 collective-permute-start
  75.1 0.6 convert_reduce_fusion
  75.7 0.2 copy.20
  75.9 0.1 pad.6.clone
  75.9 0.1 pad.3.clone
  76.0 0.0 collective-permute-done
  76.0 0.1 maximum_convert_fusion
  76.2 0.0 copy-start.8
  76.2 0.7 divide_multiply_fusion
  76.9 0.4 copy-done.8
  77.3 1.1 convolution_convert_fusion.2.part_ref
  78.4 16.2 %dt_reduce.1.low_ref = bf16[256,384]{1,0:T(8,128)(2,1)} custom-call(bf16[256,384]{1,0:T(8,128)(2,1)} %convolution_convert_fusion.2.part_ref, f32[1,256]{1,0:T(1,128)} %bitcast.42), custom_call_target="tpu_custom_call" | custom-call | bytes 30000000 | tf_op jit(solution)/shard_map/dt_reduce/pallas_call | solution.py:90
  94.7 0.0 copy-done.2
  94.7 39.0 %scan.1 = f32[256,1024]{1,0:T(8,128)} custom-call(bf16[256,384]{1,0:T(8,128)(2,1)} %dt_reduce.1.low_ref, bf16[256,1024]{1,0:T(8,128)(2,1)} %proj_ref.1, f32[1,1024]{1,0:T(1,128)} %bitcast.37, f32[256,1024]{1,0:T(8,128)} %bitcast.28, f32[16,1024]{1,0:T(8,128)} %bitcast.32), custom_call_target="tpu_custom_call" | custom-call | bytes 90000000 | tf_op jit(solution)/shard_map/scan/pallas_call | solution.py:257
  133.7 0.0 all-gather.6.cloned.1.call-done
  133.7 6.9 %fusion.11.gated_ref = bf16[256,1024]{1,0:T(8,128)(2,1)} fusion(f32[256,1024]{1,0:T(8,128)} %scan.1, bf16[4096,1024]{1,0:T(8,128)(2,1)} %all-gather.6.cloned.1.call-done, bf16[256,4096]{1,0:T(8,128)(2,1)S(1)} %bitcast.26, f32[4096]{0:T(1024)S(1)} %copy-done.9, f32[256]{0:T(256)S(1)} %rsqrt_bitcast_fusion), kind=kOutput, calls=%fused_computation.22 | convolution fusion | flops 2153775104 | bytes 12076032 | tf_op jit(solution)/shard_map/dot_general | solution.py:459
  140.6 101.9 %out_reduce.1 = bf16[256,4096]{1,0:T(8,128)(2,1)} custom-call(bf16[256,1024]{1,0:T(8,128)(2,1)} %fusion.11.gated_ref, bf16[1024,4096]{1,0:T(8,128)(2,1)} %w_ref.1, bf16[256,4096]{1,0:T(8,128)(2,1)} %bitcast.24), custom_call_target="tpu_custom_call" | custom-call | bytes 180000000 | tf_op jit(solution)/shard_map/out_reduce/pallas_call | solution.py:345
  242.5 0.0 copy-start
  242.5 0.0 copy-start.10
  242.5 2.0 constant_dynamic-slice_fusion
  244.6 2.1 fusion
  246.7 0.0 all-gather.8.cloned.1.call-done
  246.7 9.7 %fusion.24 = (f32[256]{0:T(256)S(1)}, f32[256,2048]{1,0:T(8,128)}) fusion(bf16[2048,4096]{1,0:T(8,128)(2,1)} %all-gather.8.cloned.1.call-done, bf16[256,4096]{1,0:T(8,128)(2,1)S(1)} %copy-done, f32[4096]{0:T(1024)S(1)} %copy-done.10, f32[256]{0:T(256)S(1)} %add_rsqrt_fusion), kind=kOutput, calls=%fused_computation.49 | convolution fusion | flops 4299685888 | bytes 20989952 | tf_op jit(solution)/shard_map/dot_general | solution.py:468
  256.4 2.2 exponential_reduce_fusion
  258.6 0.7 maximum_maximum_fusion.stats_ref
  259.3 23.2 %tail.1 = (f32[1,256]{1,0:T(1,128)}, f32[8,128]{1,0:T(8,128)}) custom-call(f32[8,256]{1,0:T(8,128)} %maximum_maximum_fusion.stats_ref, f32[1,256]{1,0:T(1,128)} %bitcast.41), custom_call_target="tpu_custom_call" | custom-call | bytes 18000000 | tf_op jit(solution)/shard_map/tail/pallas_call | solution.py:398
  282.5 1.2 slice.39
  285.0 1.2 copy.22
  (15 shorter events, 0.1 us)
Async XLA Ops:
  7.2 2.3 copy-start.1
  7.2 59.7 %all-gather.4.cloned.1.call-start = ((), (), s32[]{:S(2)}) async-start(), calls=%async_computation | async-start | bytes 9437184 | tf_op jit(solution)/shard_map/all_gather | solution.py:430
  7.9 125.8 %all-gather.6.cloned.1.call-start = ((), (), s32[]{:S(2)}) async-start(), calls=%async_computation.1 | async-start | bytes 9437184 | tf_op jit(solution)/shard_map/all_gather | solution.py:432
  8.7 1.3 copy-start.6
  8.7 1.3 copy-start.7
  8.7 2.0 copy-start.4
  8.7 58.2 %copy-start.9 = (f32[4096]{0:T(1024)S(1)}, f32[4096]{0:T(1024)}, u32[]{:S(2)}) copy-start(f32[4096]{0:T(1024)} %param.18) | copy-start | bytes 49156
  8.7 238.0 %all-gather.8.cloned.1.call-start = ((), (), s32[]{:S(2)}) async-start(), calls=%async_computation.2 | async-start | bytes 18874368 | tf_op jit(solution)/shard_map/all_gather | solution.py:433
  66.9 8.8 %copy-start.3 = (bf16[1024,32]{0,1:T(8,128)(2,1)S(1)}, bf16[1024,32]{0,1:T(8,128)(2,1)}, u32[]{:S(2)}) copy-start(bf16[1024,32]{0,1:T(8,128)(2,1)} %param.24) | copy-start | bytes 196612
  66.9 9.3 %copy-start.5 = (f32[1024]{0:T(1024)S(1)}, f32[1024]{0:T(1024)}, u32[]{:S(2)}) copy-start(f32[1024]{0:T(1024)} %param.22) | copy-start | bytes 12292
  72.7 3.3 %collective-permute-start = (bf16[2,3,1024]{2,1,0:T(4,128)(2,1)S(1)}, bf16[2,3,1024]{2,1,0:T(4,128)(2,1)S(1)}, u32[]{:S(2)}, u32[]{:S(2)}) collective-permute-start(bf16[2,3,1024]{2,1,0:T(4,128)(2,1)S(1)} %slice.40), channel_id=1, source_target_pairs={{0,4},{4,8},{8,12},{12,16},{16,20},{20,24},{24,28},{1,5},{5,9},{9,... | collective-permute-start | bytes 36872 | tf_op jit(solution)/shard_map/ppermute | solution.py:445
  76.2 1.1 copy-start.8
  76.9 17.8 %copy-start.2 = (f32[2,128,1024]{2,1,0:T(8,128)}, f32[2,128,1024]{2,1,0:T(8,128)S(1)}, u32[]{:S(2)}) copy-start(f32[2,128,1024]{2,1,0:T(8,128)S(1)} %divide_multiply_fusion) | copy-start | bytes 3145732
  242.5 4.2 %copy-start = (bf16[256,4096]{1,0:T(8,128)(2,1)S(1)}, bf16[256,4096]{1,0:T(8,128)(2,1)}, u32[]{:S(2)}) copy-start(bf16[256,4096]{1,0:T(8,128)(2,1)} %out_reduce.1) | copy-start | bytes 6291460
  242.5 4.2 %copy-start.10 = (f32[4096]{0:T(1024)S(1)}, f32[4096]{0:T(1024)}, u32[]{:S(2)}) copy-start(f32[4096]{0:T(1024)} %param.30) | copy-start | bytes 49156
Sparse Core Ops, SparseCore 0:
  9.9 56.9 all-gather.3
  68.8 57.0 all-gather.5
  127.8 96.5 all-gather.7
where the time goes:
time: 294 us
  Pallas kernels  180 us (61%)
  waiting for transfers between devices  58.3 us (20%)
  matrix products  23.5 us (8%)
  between operations  16.4 us (6%)
  other arithmetic  7.55 us (3%)
  local copies, waits for them, and re-layouts  5.26 us (2%)
    pallas_call x1, Pallas kernels, out_reduce(): call(functools.partial(out_kernel, nv), jax.ShapeDtypeStruct((rows, width...  102 us
    all_gather x1, waiting for transfers between devices, body(): full_x = lax.all_gather(in_x, 'dp', axis=0, tiled=True)  56.2 us
    pallas_call x1, Pallas kernels, scan(): call(functools.partial(scan_kernel, nd, batch, nstate, ranks), jax.ShapeD...  39 us
    pallas_call x1, Pallas kernels, tail(): call(functools.partial(tail_kernel, nv, nd), (jax.ShapeDtypeStruct((1, ro...  23.2 us
    pallas_call x1, Pallas kernels, dt_reduce(): call(functools.partial(dt_kernel, nv, ranks), jax.ShapeDtypeStruct((rows,...  16.2 us
    dot_general x1, matrix products, body(): lax.dot_general(final, full_head, (((1,), (1,)), ((), ())), preferred_ele...  9.69 us
    dot_general x1, matrix products, body(): jnp.dot(normed, full_z, preferred_element_type=jnp.float32)  6.91 us
  transfers between devices with their start and end apart: 4, of which 1 were waited for; matrix products, arithmetic and copies ran while one was open for 7% of the time, Pallas kernels for 53%

commit v1 on v0

--- a/solution.py
+++ b/solution.py
@@ -272,142 +272,430 @@
     )(low, proj, bias, conv, rate)
 
 
-def out_kernel(nv, gated_ref, w_ref, resid_ref, out_ref, sent, recv, mine, s1, r1, s2, r2):
+def back_kernel(
+    nv, nd, steps, relay_at, gated_ref, w_ref, resid_ref, gain_ref, head_ref, ids_ref, mask_ref,
+    hidden_ref, logp_ref, sum_ref,
+    weight, own, near, send_up, recv_up, send_down, recv_down, hid, fin, full, logits, ids, stats, heard,
+    part, parts, w_sem, near_sem, up_s, up_r, down_s, down_r, gup_s, gup_r, gdown_s, gdown_r,
+    fin_s, fin_r, ids_s, ids_r, head_l, head_s, head_r, pass_s, pass_r, stat_s, stat_r, sum_s, sum_r,
+):
     me = lax.axis_index("vocab")
-    rows, width = resid_ref.shape
+    dev = lax.axis_index("dp")
+    chip, core = dev // 2, lax.rem(dev, 2)
+    mate = {"dp": chip * 2 + 1 - core}
+    above, below = {"vocab": lax.rem(me + 1, nv)}, {"vocab": lax.rem(me + nv - 1, nv)}
+    rows, chans = gated_ref.shape
+    width = w_ref.shape[1]
     share = width // nv
-    greet(("vocab",))
-
-    def columns(index):
-        return pl.ds(pl.multiple_of(index * share, share), share)
+    entries, feats = head_ref.shape
+    half = entries // 2
+    size = rows // steps
+
+    def block(index, length):
+        return pl.ds(pl.multiple_of(index * length, length), length)
+
+    weight_copies = []
+    for s in range(nv):
+        index = jnp.where(me * 2 < nv, nv - 1 - s, s)
+        copy = pltpu.make_async_copy(
+            w_ref.at[:, block(index, share)], weight.at[:, block(index, share)], w_sem.at[s]
+        )
+        copy.start()
+        weight_copies.append((index, copy))
+    near_copy = pltpu.make_async_copy(resid_ref.at[:, block(me, share)], near, near_sem)
+    near_copy.start()
+    greet_back(nv, nd)
+
+    head_waits, head_sends, passes = gather_halves(
+        nd, lambda c: head_ref.at[block(c, half)], lambda d: full.at[:, block(d, feats)], half,
+        head_l, head_s, head_r, pass_s, pass_r,
+    )
+    mine = ids.at[core]
+    ids[core] = ids_ref[...]
+    ids_copy = remote(ids_ref, mine, ids_s, ids_r, mate)
+    ids_copy.start()
+
+    def up(i, j):
+        return remote(send_up.at[i, j - 1], recv_up.at[i, j - 1], up_s.at[i, j - 1], up_r.at[i, j - 1], above)
+
+    def down(i, j):
+        return remote(send_down.at[i, j], recv_down.at[i, j], down_s.at[i, j], down_r.at[i, j], below)
+
+    def spread_up(i, s):
+        at = hid.at[block(i, size), block(s, share)]
+        return remote(at, at, gup_s.at[i, s], gup_r.at[i, s], above)
+
+    def spread_down(i, s):
+        at = hid.at[block(i, size), block(s, share)]
+        return remote(at, at, gdown_s.at[i, s - 1], gdown_r.at[i, s - 1], below)
+
+    def fin_copy(i):
+        at = fin.at[core, block(i, size)]
+        return remote(at, at, fin_s.at[i], fin_r.at[i], mate)
 
     tile = min(512, share)
-
-    def product(index, put):
+    for index, copy in weight_copies:
+        copy.wait()
+
         @pl.loop(0, share // tile)
         def _(k):
-            at = pl.multiple_of(index * share + k * tile, tile)
-            put(
-                pl.ds(pl.multiple_of(k * tile, tile), tile), pl.ds(at, tile),
-                jnp.dot(
-                    gated_ref[...], w_ref[:, pl.ds(at, tile)], preferred_element_type=jnp.float32
-                ),
+            at = pl.ds(pl.multiple_of(index * share + k * tile, tile), tile)
+            own[:, at] = jnp.dot(gated_ref[...], weight[:, at], preferred_element_type=jnp.float32)
+
+        @pl.when((me == 0) & (index > 0))
+        def _():
+            @pl.loop(0, steps)
+            def _(i):
+                send_up[i, index - 1] = own[block(i, size), block(index, share)].astype(jnp.bfloat16)
+                up(i, index).start()
+
+        @pl.when((me == nv - 1) & (index < nv - 1))
+        def _():
+            @pl.loop(0, steps)
+            def _(i):
+                send_down[i, index] = own[block(i, size), block(index, share)].astype(jnp.bfloat16)
+                down(i, index).start()
+
+    near_copy.wait()
+
+    def combine_up(i):
+        for j in range(nv - 1, 0, -1):
+            @pl.when((me > 0) & (me < j))
+            def _():
+                up(i, j).wait_recv()
+                send_up[i, j - 1] = (
+                    own[block(i, size), pl.ds(j * share, share)] + recv_up[i, j - 1].astype(jnp.float32)
+                ).astype(jnp.bfloat16)
+                up(i, j).start()
+
+    def combine_down(i):
+        for j in range(nv - 1):
+            @pl.when((me < nv - 1) & (me > j))
+            def _():
+                down(i, j).wait_recv()
+                send_down[i, j] = (
+                    own[block(i, size), pl.ds(j * share, share)] + recv_down[i, j].astype(jnp.float32)
+                ).astype(jnp.bfloat16)
+                down(i, j).start()
+
+    def finish(i):
+        at = block(i, size)
+        own[at, block(me, share)] = own[at, block(me, share)] + near[at, :].astype(jnp.float32)
+
+        @pl.when(me > 0)
+        def _():
+            up(i, me).wait_recv()
+            own[at, block(me, share)] = own[at, block(me, share)] + recv_up[i, me - 1].astype(jnp.float32)
+
+        @pl.when(me < nv - 1)
+        def _():
+            down(i, me).wait_recv()
+            own[at, block(me, share)] = own[at, block(me, share)] + recv_down[i, me].astype(jnp.float32)
+
+        value = own[at, block(me, share)].astype(jnp.bfloat16)
+        hidden_ref[at, :] = value
+        hid[at, block(me, share)] = value
+
+        @pl.when(me < nv - 1)
+        def _():
+            spread_up(i, me).start()
+
+        @pl.when(me > 0)
+        def _():
+            spread_down(i, me).start()
+
+    def forward(i, hops):
+        low, high = me - hops, me + hops
+
+        @pl.when(low >= 0)
+        def _():
+            spread_up(i, low).wait_recv()
+
+            @pl.when(me < nv - 1)
+            def _():
+                spread_up(i, low).start()
+
+        @pl.when(high < nv)
+        def _():
+            spread_down(i, high).wait_recv()
+
+            @pl.when(me > 0)
+            def _():
+                spread_down(i, high).start()
+
+    def normalize(i):
+        at = block(i, size)
+        wide = hid[at, :].astype(jnp.float32)
+        scale = lax.rsqrt(jnp.mean(wide * wide, axis=-1, keepdims=True) + 1e-05)
+        fin[core, at] = (wide * scale * gain_ref[...]).astype(jnp.bfloat16)
+        fin_copy(i).start()
+
+    late = jnp.where(me * 2 >= nv, 1, 0)
+
+    def walk(first, last):
+        @pl.loop(first, last)
+        def _(t):
+            def at(i, step):
+                @pl.when((i >= 0) & (i < steps))
+                def _():
+                    step(i)
+
+            at(t - late, combine_up)
+            at(t - 1 + late, combine_down)
+            at(t - 2, finish)
+            for hops in range(1, nv):
+                at(t - 2 - hops, functools.partial(forward, hops=hops))
+            at(t - 1 - nv, normalize)
+
+    walk(0, relay_at)
+    passes()
+    walk(relay_at, steps + nv + 1)
+
+    @pl.loop(0, steps)
+    def _(i):
+        remote(
+            fin.at[core, block(i, size)], fin.at[1 - core, block(i, size)], fin_s.at[i], fin_r.at[i], mate
+        ).wait_recv()
+    ids_copy.wait()
+    head_waits()
+
+    vt = min(256, half)
+    for s in range(2):
+        @pl.loop(0, half // vt)
+        def _(k):
+            logits[block(k, vt), s * rows : (s + 1) * rows] = lax.dot_general(
+                full[block(k, vt), :], fin[s], (((1,), (1,)), ((), ())), preferred_element_type=jnp.float32
             )
 
-    copies = {}
-    order = sorted(range(1, nv), key=lambda s: abs(s - nv / 2))
-    for shift in order:
-        def put(local, whole, value):
-            sent[shift - 1, :, local] = value.astype(jnp.bfloat16)
-
-        product(lax.rem(me + shift, nv), put)
-        copy = remote(
-            sent.at[shift - 1], recv.at[shift - 1],
-            s1.at[shift - 1], r1.at[shift - 1], peer("vocab", shift),
-        )
-        copy.start()
-        copies[shift] = copy
-
-    def put(local, whole, value):
-        mine[:, local] = value
-
-    product(me, put)
-    for shift in order:
-        copies[shift].wait()
-
-    @pl.loop(0, share // tile)
-    def _(k):
-        local = pl.ds(pl.multiple_of(k * tile, tile), tile)
-        whole = pl.ds(pl.multiple_of(me * share + k * tile, tile), tile)
-        total = mine[:, local]
-        for shift in range(1, nv):
-            total = total + recv[shift - 1, :, local].astype(jnp.float32)
-        hidden = (resid_ref[:, whole].astype(jnp.float32) + total).astype(jnp.bfloat16)
-        sent[nv - 1, :, local] = hidden
-        out_ref[:, whole] = hidden
-
-    copies = []
-    for shift in range(1, nv):
-        copy = remote(
-            sent.at[nv - 1], out_ref.at[:, columns(me)],
-            s2.at[shift - 1], r2.at[shift - 1], peer("vocab", shift),
-        )
-        copy.start()
-        copies.append(copy)
-    for copy in copies:
-        copy.wait()
-
-
-def out_reduce(gated, w, resid, nv):
-    rows, width = resid.shape
-    share = width // nv
-    sems = [pltpu.SemaphoreType.DMA((nv - 1,))] * 4
-    return call(
-        functools.partial(out_kernel, nv),
-        jax.ShapeDtypeStruct((rows, width), jnp.bfloat16),
-        [
-            pltpu.VMEM((nv, rows, share), jnp.bfloat16),
-            pltpu.VMEM((nv - 1, rows, share), jnp.bfloat16),
-            pltpu.VMEM((rows, share), jnp.float32),
-        ] + sems,
-        3, 60, "out_reduce",
-    )(gated, w, resid)
-
-
-def tail_kernel(nv, nd, stats_ref, mask_ref, logp_ref, sum_ref, recv, part, parts, s1, r1, s2, r2):
-    greet(("vocab", "dp"))
-    copies = []
-    for shift in range(1, nv):
-        copy = remote(
-            stats_ref, recv.at[shift - 1], s1.at[shift - 1], r1.at[shift - 1],
-            peer("vocab", shift),
-        )
-        copy.start()
-        copies.append(copy)
-    for copy in copies:
-        copy.wait()
-    everyone = [stats_ref[...]] + [recv[k] for k in range(nv - 1)]
+        def highest(k, top):
+            return jnp.maximum(
+                top, jnp.max(logits[block(k, vt), s * rows : (s + 1) * rows], axis=0, keepdims=True)
+            )
+
+        top = lax.fori_loop(0, half // vt, highest, jnp.full((1, rows), -jnp.inf, jnp.float32))
+        wanted = ids[s, 0:1, :] - (me * entries + core * half)
+
+        def gather(k, carry):
+            total, picked = carry
+            values = logits[block(k, vt), s * rows : (s + 1) * rows]
+            entry = lax.broadcasted_iota(jnp.int32, values.shape, 0) + k * vt
+            total = total + jnp.sum(jnp.exp(values - top), axis=0, keepdims=True)
+            picked = picked + jnp.sum(jnp.where(entry == wanted, values, 0.0), axis=0, keepdims=True)
+            return total, picked
+
+        zero = jnp.zeros((1, rows), jnp.float32)
+        total, picked = lax.fori_loop(0, half // vt, gather, (zero, zero))
+        stats[s, 0:1, :] = top
+        stats[s, 1:2, :] = total
+        stats[s, 2:3, :] = picked
+        stats[s, 3:8, :] = jnp.zeros((5, rows), jnp.float32)
+
+    sends = []
+    for shift in range(nv):
+        for other in range(2):
+            if shift == 0 and other == 0:
+                continue
+            owner = core if other == 0 else 1 - core
+            copy = remote(
+                stats.at[owner], heard.at[me, core], stat_s.at[shift, other], stat_r.at[me, core],
+                {"vocab": lax.rem(me + shift, nv), "dp": chip * 2 + owner},
+            )
+            copy.start()
+            sends.append(copy)
+    heard[me, core] = stats[core]
+    for z in range(nv):
+        for c in range(2):
+            @pl.when((z != me) | (c != core))
+            def _():
+                remote(stats.at[0], heard.at[z, c], stat_s.at[0, 1], stat_r.at[z, c], mate).wait_recv()
+    everyone = [heard[z, c] for z in range(nv) for c in range(2)]
     top = everyone[0][0:1]
-    for stats in everyone[1:]:
-        top = jnp.maximum(top, stats[0:1])
+    for one in everyone[1:]:
+        top = jnp.maximum(top, one[0:1])
     total = jnp.zeros_like(top)
     picked = jnp.zeros_like(top)
-    for stats in everyone:
-        total = total + stats[1:2] * jnp.exp(stats[0:1] - top)
-        picked = picked + stats[2:3]
+    for one in everyone:
+        total = total + one[1:2] * jnp.exp(one[0:1] - top)
+        picked = picked + one[2:3]
     logp = picked - (top + jnp.log(total))
     logp_ref[...] = logp
     masked = jnp.sum(jnp.where(mask_ref[...] > 0.0, logp, 0.0), axis=-1, keepdims=True)
     part[...] = jnp.broadcast_to(masked, part.shape)
-    copies = []
     for shift in range(1, nd):
         copy = remote(
-            part, parts.at[shift - 1], s2.at[shift - 1], r2.at[shift - 1], peer("dp", shift)
+            part, parts.at[dev], sum_s.at[shift - 1], sum_r.at[dev], {"dp": lax.rem(dev + shift, nd)}
         )
         copy.start()
-        copies.append(copy)
-    grand = part[...]
+        sends.append(copy)
+    parts[dev] = part[...]
+    for d in range(nd):
+        @pl.when(d != dev)
+        def _():
+            remote(part, parts.at[d], sum_s.at[0], sum_r.at[d], mate).wait_recv()
+    grand = parts[0]
+    for d in range(1, nd):
+        grand = grand + parts[d]
+    sum_ref[...] = grand
+
+    for copy in sends:
+        copy.wait_send()
+    head_sends()
+
+    @pl.loop(0, steps)
+    def _(i):
+        fin_copy(i).wait_send()
+        for j in range(1, nv):
+            @pl.when(me < j)
+            def _():
+                up(i, j).wait_send()
+        for j in range(nv - 1):
+            @pl.when(me > j)
+            def _():
+                down(i, j).wait_send()
+        for s in range(nv - 1):
+            @pl.when((me >= s) & (me < nv - 1))
+            def _():
+                spread_up(i, s).wait_send()
+        for s in range(1, nv):
+            @pl.when((me <= s) & (me > 0))
+            def _():
+                spread_down(i, s).wait_send()
+
+
+def greet_back(nv, nd):
+    barrier = pltpu.get_barrier_semaphore()
+    me, dev = lax.axis_index("vocab"), lax.axis_index("dp")
+    mate = dev // 2 * 2 + 1 - lax.rem(dev, 2)
     for shift in range(1, nd):
-        copies[shift - 1].wait()
-        grand = grand + parts[shift - 1]
-    sum_ref[...] = grand
-
-
-def tail(stats, mask, nv, nd):
-    rows = stats.shape[1]
-    return call(
-        functools.partial(tail_kernel, nv, nd),
-        (
+        pl.semaphore_signal(barrier, inc=1, device_id=peer("dp", shift), device_id_type=MESH)
+    for shift in range(1, nv):
+        z = lax.rem(me + shift, nv)
+        pl.semaphore_signal(barrier, inc=1, device_id={"vocab": z}, device_id_type=MESH)
+        pl.semaphore_signal(barrier, inc=1, device_id={"vocab": z, "dp": mate}, device_id_type=MESH)
+    pl.semaphore_wait(barrier, nd - 1 + 2 * (nv - 1))
+
+
+def gather_halves(nd, source, target, length, local, send, recv, pass_s, pass_r):
+    dev = lax.axis_index("dp")
+    chip, core = dev // 2, lax.rem(dev, 2)
+    keep = pltpu.make_async_copy(source(core), target(dev), local)
+    keep.start()
+    copies = [remote(source(1 - core), target(dev), send.at[0, 0], recv.at[0, core], {"dp": chip * 2 + 1 - core})]
+    copies[0].start()
+    waits = [remote(source(0), target(chip * 2 + 1 - core), send.at[0, 0], recv.at[0, 1 - core], {"dp": dev})]
+    if nd != 8:
+        for shift in range(1, nd // 2):
+            there = lax.rem(chip + shift, nd // 2)
+            back = lax.rem(chip + nd // 2 - shift, nd // 2)
+            for c in range(2):
+                copy = remote(
+                    source(c), target(dev), send.at[shift, c], recv.at[shift, core], {"dp": there * 2 + c}
+                )
+                copy.start()
+                copies.append(copy)
+                waits.append(
+                    remote(source(c), target(back * 2 + c), send.at[shift, c], recv.at[shift, c], {"dp": dev})
+                )
+        passes = lambda: None
+    else:
+        piece = length // 2
+        sides = (chip + 1 - 2 * lax.rem(chip, 2), lax.rem(chip + 2, 4))
+
+        def at(ref, p):
+            return ref.at[pl.ds(p * piece, piece)]
+
+        first = []
+        for turn in range(2):
+            for side in range(2):
+                p = side if turn == 0 else 1 - side
+                for c in range(2):
+                    k = 1 + side * 2 + p
+                    copy = remote(
+                        at(source(c), p), at(target(dev), p), send.at[k, c], recv.at[k, core],
+                        {"dp": sides[side] * 2 + c},
+                    )
+                    copy.start()
+                    copies.append(copy)
+                    came = at(target(sides[side] * 2 + c), p)
+                    wait = remote(came, came, send.at[k, c], recv.at[k, c], {"dp": dev})
+                    if turn == 0:
+                        first.append((side, p, c, wait, came))
+                    else:
+                        waits.append(wait)
+
+        far = 3 - chip
+        for side in range(2):
+            for c in range(2):
+                came = at(target(far * 2 + c), 1 - side)
+                waits.append(
+                    remote(came, came, pass_s.at[side, c], pass_r.at[1 - side, c], {"dp": dev})
+                )
+
+        def passes():
+            for side, p, c, wait, came in first:
+                wait.wait_recv()
+                copy = remote(
+                    came, came, pass_s.at[side, c], pass_r.at[p, c], {"dp": sides[1 - side] * 2 + core}
+                )
+                copy.start()
+                copies.append(copy)
+
+    def finish_waits():
+        keep.wait()
+        for wait in waits:
+            wait.wait_recv()
+
+    def finish_sends():
+        for copy in copies:
+            copy.wait_send()
+
+    return finish_waits, finish_sends, passes
+
+
+def back(gated, w, resid, gain, head, ids, mask, nv, nd, steps=4, relay_at=3):
+    rows, chans = gated.shape
+    width = w.shape[1]
+    share = width // nv
+    half = head.shape[0] // 2
+    size = rows // steps
+    dma = pltpu.SemaphoreType.DMA
+    line = pltpu.VMEM((steps, nv - 1, size, share), jnp.bfloat16)
+    lanes = 5 if nd == 8 else nd // 2
+    anywhere = pl.BlockSpec(memory_space=pl.ANY)
+    return pl.pallas_call(
+        functools.partial(back_kernel, nv, nd, steps, relay_at),
+        out_shape=(
+            jax.ShapeDtypeStruct((rows, share), jnp.bfloat16),
             jax.ShapeDtypeStruct((1, rows), jnp.float32),
-            jax.ShapeDtypeStruct((8, 128), jnp.float32),
+            jax.ShapeDtypeStruct((8, LANE), jnp.float32),
         ),
-        [
-            pltpu.VMEM((nv - 1, 8, rows), jnp.float32),
-            pltpu.VMEM((8, 128), jnp.float32),
-            pltpu.VMEM((nd - 1, 8, 128), jnp.float32),
-        ] + [pltpu.SemaphoreType.DMA((nv - 1,))] * 2 + [pltpu.SemaphoreType.DMA((nd - 1,))] * 2,
-        4, 6, "tail",
-    )(stats, mask)
+        in_specs=[VMEM, anywhere, anywhere, VMEM, anywhere, VMEM, VMEM],
+        out_specs=(VMEM, VMEM, VMEM),
+        scratch_shapes=[
+            pltpu.VMEM((chans, width), jnp.bfloat16),
+            pltpu.VMEM((rows, width), jnp.float32),
+            pltpu.VMEM((rows, share), jnp.bfloat16),
+            line, line, line, line,
+            pltpu.VMEM((rows, width), jnp.bfloat16),
+            pltpu.VMEM((2, rows, width), jnp.bfloat16),
+            pltpu.VMEM((half, width), jnp.bfloat16),
+            pltpu.VMEM((half, 2 * rows), jnp.float32),
+            pltpu.VMEM((2, 8, rows), jnp.int32),
+            pltpu.VMEM((2, 8, rows), jnp.float32),
+            pltpu.VMEM((nv, 2, 8, rows), jnp.float32),
+            pltpu.VMEM((8, LANE), jnp.float32),
+            pltpu.VMEM((nd, 8, LANE), jnp.float32),
+            dma((nv,)), dma,
+        ] + [dma((steps, nv - 1))] * 8 + [
+            dma((steps,)), dma((steps,)), dma, dma, dma, dma((lanes, 2)), dma((lanes, 2)),
+            dma((2, 2)), dma((2, 2)), dma((nv, 2)), dma((nv, 2)), dma((nd,)), dma((nd,)),
+        ],
+        compiler_params=pltpu.CompilerParams(
+            collective_id=3, has_side_effects=True, vmem_limit_bytes=60 * 1024 * 1024
+        ),
+        cost_estimate=pl.CostEstimate(flops=0, bytes_accessed=int(80 * 3.0e6), transcendentals=0),
+        name="back",
+    )(gated, w, resid, gain, head, ids, mask)
 
 
 def rms_norm(values, gain, epsilon):
@@ -425,12 +713,10 @@
     ranks = xdt_w.shape[1]
     kernel_len = conv_w.shape[0]
     rows = batch * local_len
-    vocab_index = lax.axis_index("vocab")
 
     full_x = lax.all_gather(in_x, "dp", axis=0, tiled=True)
     in_z, _ = lax.optimization_barrier((in_z, in_x))
     full_z = lax.all_gather(in_z, "dp", axis=0, tiled=True)
-    full_head = lax.all_gather(head_w, "dp", axis=1, tiled=True)
 
     pad = -(2 * nstate) % 128
     low_w = jnp.concatenate([xdt_w, xbc_w, jnp.zeros((channels, pad), jnp.bfloat16)], axis=1)
@@ -461,25 +747,11 @@
         .astype(jnp.float32)
     )
     gated = (mixed * jax.nn.silu(z_gate)).astype(jnp.bfloat16)
-    hidden = out_reduce(gated, out_w, flat, nv)
     share = width // nv
-    hidden_share = lax.dynamic_slice_in_dim(hidden, vocab_index * share, share, 1)
-    final = rms_norm(hidden.astype(jnp.float32), final_gain, 1e-05).astype(jnp.bfloat16)
-    logits = lax.dot_general(
-        final, full_head, (((1,), (1,)), ((), ())), preferred_element_type=jnp.float32
-    )
-    vocab_rows = head_w.shape[0]
-    local_ids = targets.reshape(rows) - vocab_index * vocab_rows
-    entry_ids = lax.broadcasted_iota(jnp.int32, (rows, vocab_rows), 1)
-    picked = jnp.sum(jnp.where(entry_ids == local_ids[:, None], logits, 0.0), axis=-1)
-    top = jnp.max(logits, axis=-1)
-    total = jnp.sum(jnp.exp(logits - top[:, None]), axis=-1)
-    stats = jnp.concatenate(
-        [top[None], total[None], picked[None], jnp.zeros((5, rows), jnp.float32)], axis=0
-    )
     positions = lax.axis_index("dp") * local_len + jnp.arange(local_len, dtype=jnp.int32)
     mask = (positions[None, :] < lengths[:, None]).astype(jnp.float32).reshape(1, rows)
-    logp, grand = tail(stats, mask, nv, nd)
+    ids = jnp.broadcast_to(targets.reshape(1, rows), (8, rows))
+    hidden_share, logp, grand = back(gated, out_w, flat, final_gain[None, :], head_w, ids, mask, nv, nd)
     mean_logp = grand[0, 0] / jnp.sum(lengths.astype(jnp.float32))
     return (
         hidden_share.reshape(batch, local_len, share),

time: 294 us -> 260 us (0.88)
  Pallas kernels: 180 us -> 160 us
  matrix products: 23.5 us -> 13.9 us
  other arithmetic: 7.55 us -> 2.58 us
    pallas_call x2 -> x1, Pallas kernels: 125 us -> 105 us  [back(): pl.pallas_call(functools.partial(back_kernel, nv, nd, steps, relay_at), o...]
    dot_general x1 -> x0, matrix products: 9.69 us -> none  [body(): lax.dot_general(final, full_head, (((1,), (1,)), ((), ())), preferred_ele...]
  transfers between devices with their start and end apart: 4 -> 3, of which waited for: 1 -> 1; matrix products, arithmetic and copies ran while one was open for 7% -> 4% of each run, Pallas kernels for 53% -> 21%
where the time goes in v1:
time: 260 us
  Pallas kernels  160 us (62%)
  waiting for transfers between devices  58.4 us (22%)
  between operations  16.7 us (6%)
  matrix products  13.9 us (5%)
  local copies, waits for them, and re-layouts  5.67 us (2%)
    pallas_call x1, Pallas kernels, back(): pl.pallas_call(functools.partial(back_kernel, nv, nd, steps, relay_at), o...  105 us
    all_gather x1, waiting for transfers between devices, body(): full_x = lax.all_gather(in_x, 'dp', axis=0, tiled=True)  57 us
    pallas_call x1, Pallas kernels, scan(): call(functools.partial(scan_kernel, nd, batch, nstate, ranks), jax.ShapeD...  39.4 us
    pallas_call x1, Pallas kernels, dt_reduce(): call(functools.partial(dt_kernel, nv, ranks), jax.ShapeDtypeStruct((rows,...  16.3 us
    dot_general x1, matrix products, body(): jnp.dot(normed, full_z, preferred_element_type=jnp.float32)  6.94 us
    dot_general x1, matrix products, body(): jnp.dot(normed, full_x, preferred_element_type=jnp.float32)  5.8 us
  transfers between devices with their start and end apart: 3, of which 1 were waited for; matrix products, arithmetic and copies ran while one was open for 4% of the time, Pallas kernels for 21%

profile of v1, /device:TPU:0, one launch (start us, length us, event | category | flops | bytes accessed | tf_op | source)
XLA Modules:
  0.0 259.8 jit_solution(13248364263815728183)
XLA Ops:
  7.2 0.0 copy-start
  7.2 0.0 copy-start.6
  7.2 0.0 copy-start.3
  7.2 0.0 copy-start.8
  7.2 0.0 all-gather.3.cloned.1.call-start
  7.3 0.7 all-gather.3.cloned.1.call-update
  7.9 0.0 all-gather.5.cloned.1.call-start
  8.0 0.7 all-gather.5.cloned.1.call-update
  8.7 0.1 copy-done
  8.8 0.5 multiply_reduce_fusion
  9.3 0.0 copy-done.6
  9.3 0.6 compare_convert_fusion
  9.9 0.0 copy-done.3
  9.9 57.0 %all-gather.3.cloned.1.call-done = bf16[4096,1024]{1,0:T(8,128)(2,1)} async-done(((bf16[512,1024]{1,0:T(8,128)(2,1)}), bf16[4096,1024]{1,0:T(8,128)(2,1)}) %all-gather.3.cloned.1.call-update) | async-done | bytes 8388624 | tf_op jit(solution)/shard_map/all_gather | solution.py:717
  66.9 0.0 copy-done.8
  66.9 0.0 copy-start.2
  66.9 0.0 copy-start.4
  66.9 5.8 %convolution_convert_fusion.1 = bf16[256,1024]{1,0:T(8,128)(2,1)S(1)} fusion(bf16[4096,1024]{1,0:T(8,128)(2,1)} %all-gather.3.cloned.1.call-done, bf16[256,4096]{1,0:T(8,128)(2,1)S(1)} %bitcast.21, f32[4096]{0:T(1024)S(1)} %copy-done.8, f32[256]{0:T(256)S(1)} %rsqrt_bitcast_fusion), kind=kOutput, calls=%fused_computation.5 | convolution fusion | flops 2151940096 | bytes 11027456 | tf_op jit(solution)/shard_map/dot_general | solution.py:727
  72.8 2.1 collective-permute-start
  74.9 0.6 convert_reduce_fusion
  75.5 0.0 copy-done.2
  75.5 0.2 copy.20
  75.7 0.1 pad.2.clone
  75.8 0.0 collective-permute-done
  75.8 0.2 maximum_convert_fusion
  76.0 0.0 copy-done.4
  76.0 0.0 copy-start.7
  76.0 0.7 divide_multiply_fusion
  76.6 0.0 copy-start.1
  76.7 0.4 copy-done.7
  77.1 1.1 convolution_convert_fusion.2.part_ref
  78.2 16.3 %dt_reduce.1.low_ref = bf16[256,384]{1,0:T(8,128)(2,1)} custom-call(bf16[256,384]{1,0:T(8,128)(2,1)} %convolution_convert_fusion.2.part_ref, f32[1,256]{1,0:T(1,128)} %bitcast.36), custom_call_target="tpu_custom_call" | custom-call | bytes 30000000 | tf_op jit(solution)/shard_map/dt_reduce/pallas_call | solution.py:90
  94.5 0.0 copy-done.1
  94.5 39.4 %scan.1 = f32[256,1024]{1,0:T(8,128)} custom-call(bf16[256,384]{1,0:T(8,128)(2,1)} %dt_reduce.1.low_ref, bf16[256,1024]{1,0:T(8,128)(2,1)} %proj_ref.1, f32[1,1024]{1,0:T(1,128)} %bitcast.34, f32[256,1024]{1,0:T(8,128)} %bitcast.24, f32[16,1024]{1,0:T(8,128)} %bitcast.28), custom_call_target="tpu_custom_call" | custom-call | bytes 90000000 | tf_op jit(solution)/shard_map/scan/pallas_call | solution.py:257
  133.8 0.0 copy-start.5
  133.9 0.0 all-gather.5.cloned.1.call-done
  133.9 6.9 %fusion.4.gated_ref = bf16[256,1024]{1,0:T(8,128)(2,1)} fusion(f32[256,1024]{1,0:T(8,128)} %scan.1, bf16[4096,1024]{1,0:T(8,128)(2,1)} %all-gather.5.cloned.1.call-done, bf16[256,4096]{1,0:T(8,128)(2,1)S(1)} %bitcast.22, f32[4096]{0:T(1024)S(1)} %copy-done.8, f32[256]{0:T(256)S(1)} %rsqrt_bitcast_fusion), kind=kOutput, calls=%fused_computation.11 | convolution fusion | flops 2153775104 | bytes 12076032 | tf_op jit(solution)/shard_map/dot_general | solution.py:745
  140.8 0.0 copy-done.5
  140.8 0.6 broadcast_in_dim.29.ids_ref
  141.4 104.8 %back.1 = (bf16[256,1024]{1,0:T(8,128)(2,1)}, f32[1,256]{1,0:T(1,128)}, f32[8,128]{1,0:T(8,128)}) custom-call(bf16[256,1024]{1,0:T(8,128)(2,1)} %fusion.4.gated_ref, bf16[1024,4096]{1,0:T(8,128)(2,1)} %w_ref.1, bf16[256,4096]{1,0:T(8,128)(2,1)} %bitcast.20, f32[1,4096]{1,0:T(1,128)} %bitcast.29, bf16[2048,512]{1,0:T(8,128)(2,1)} %head_ref.1, ...), custom_call_target="tpu_custom_call" | custom-call | bytes 240000000 | tf_op jit(solution)/shard_map/back/pallas_call | solution.py:665
  246.2 1.2 slice.39
  248.7 1.9 copy.23
  250.6 1.2 copy.24
  (5 shorter events, 0.0 us)
Async XLA Ops:
  7.2 1.6 copy-start
  7.2 2.1 copy-start.6
  7.2 2.7 %copy-start.3 = (f32[4,1024]{1,0:T(4,128)S(1)}, f32[4,1024]{1,0:T(4,128)}, u32[]{:S(2)}) copy-start(f32[4,1024]{1,0:T(4,128)} %param.21) | copy-start | bytes 49156
  7.2 59.7 %copy-start.8 = (f32[4096]{0:T(1024)S(1)}, f32[4096]{0:T(1024)}, u32[]{:S(2)}) copy-start(f32[4096]{0:T(1024)} %param.18) | copy-start | bytes 49156
  7.2 59.7 %all-gather.3.cloned.1.call-start = ((), (), s32[]{:S(2)}) async-start(), calls=%async_computation | async-start | bytes 9437184 | tf_op jit(solution)/shard_map/all_gather | solution.py:717
  7.9 125.9 %all-gather.5.cloned.1.call-start = ((), (), s32[]{:S(2)}) async-start(), calls=%async_computation.1 | async-start | bytes 9437184 | tf_op jit(solution)/shard_map/all_gather | solution.py:719
  66.9 8.6 %copy-start.2 = (bf16[1024,32]{0,1:T(8,128)(2,1)S(1)}, bf16[1024,32]{0,1:T(8,128)(2,1)}, u32[]{:S(2)}) copy-start(bf16[1024,32]{0,1:T(8,128)(2,1)} %param.24) | copy-start | bytes 196612
  66.9 9.0 %copy-start.4 = (f32[1024]{0:T(1024)S(1)}, f32[1024]{0:T(1024)}, u32[]{:S(2)}) copy-start(f32[1024]{0:T(1024)} %param.22) | copy-start | bytes 12292
  72.8 3.0 %collective-permute-start = (bf16[2,3,1024]{2,1,0:T(4,128)(2,1)S(1)}, bf16[2,3,1024]{2,1,0:T(4,128)(2,1)S(1)}, u32[]{:S(2)}, u32[]{:S(2)}) collective-permute-start(bf16[2,3,1024]{2,1,0:T(4,128)(2,1)S(1)} %slice.40), channel_id=1, source_target_pairs={{0,4},{4,8},{8,12},{12,16},{16,20},{20,24},{24,28},{1,5},{5,9},{9,... | collective-permute-start | bytes 36872 | tf_op jit(solution)/shard_map/ppermute | solution.py:731
  76.0 1.1 copy-start.7
  76.6 17.8 %copy-start.1 = (f32[2,128,1024]{2,1,0:T(8,128)}, f32[2,128,1024]{2,1,0:T(8,128)S(1)}, u32[]{:S(2)}) copy-start(f32[2,128,1024]{2,1,0:T(8,128)S(1)} %divide_multiply_fusion) | copy-start | bytes 3145732
  133.8 7.0 %copy-start.5 = (s32[2,128]{1,0:T(2,128)S(1)}, s32[2,128]{1,0:T(2,128)}, u32[]{:S(2)}) copy-start(s32[2,128]{1,0:T(2,128)} %param.32) | copy-start | bytes 3076
Sparse Core Ops, SparseCore 0:
  9.9 56.9 all-gather.2
  68.8 57.0 all-gather.4

commit v2 on v1

--- a/solution.py
+++ b/solution.py
@@ -35,81 +35,167 @@
     )
 
 
-def call(kernel, out_shape, scratch, cid, cost_us, name):
-    return pl.pallas_call(
-        kernel,
-        out_shape=out_shape,
-        scratch_shapes=scratch,
-        compiler_params=pltpu.CompilerParams(
-            collective_id=cid, has_side_effects=True, vmem_limit_bytes=56 * 1024 * 1024
-        ),
-        cost_estimate=pl.CostEstimate(
-            flops=0, bytes_accessed=int(cost_us * 3.0e6), transcendentals=0
-        ),
-        name=name,
+def front_kernel(
+    nv, nd, batch, ranks, nstate, resid_ref, gain_ref, in_x_ref, in_z_ref, conv_w_ref, conv_b_ref, low_w_ref,
+    dt_gain_ref, proj_ref, bias_ref, rate_ref, gated_ref,
+    normed, full_x, full_z, made, whole, zwhole, edge, padded, act, part, low_recv, low_mine, low,
+    step, drive, maps, result, decay, spread, state, sums, agg, tot, agg_in, tot_in,
+    norm_s, norm_r, x_l, x_s, x_r, xp_s, xp_r, z_l, z_s, z_r, zp_s, zp_r,
+    swap_s, swap_r, edge_s, edge_r, zswap_s, zswap_r, l1_s, l1_r, l2_s, l2_r, s1, r1, s2, r2,
+):
+    me = lax.axis_index("dp")
+    chip, core = me // 2, lax.rem(me, 2)
+    mate = {"dp": chip * 2 + 1 - core}
+    vme = lax.axis_index("vocab")
+    rows, width = resid_ref.shape
+    feats, chans = in_x_ref.shape
+    half = chans // 2
+    length = rows // batch
+    greet(("dp", "vocab"))
+
+    def columns(c):
+        return pl.ds(pl.multiple_of(c * half, half), half)
+
+    def block(index, size):
+        return pl.ds(pl.multiple_of(index * size, size), size)
+
+    x_waits, x_sends, x_passes = gather_halves(
+        nd, lambda c: in_x_ref.at[:, columns(c)], lambda d: full_x.at[block(d, feats)], feats,
+        x_l, x_s, x_r, xp_s, xp_r,
     )
-
-
-def dt_kernel(nv, ranks, part_ref, gain_ref, out_ref, recv, mine, s1, r1, s2, r2):
-    me = lax.axis_index("vocab")
-    rows = part_ref.shape[0] // nv
-    greet(("vocab",))
+    piece = min(32, rows)
+
+    @pl.loop(0, rows // piece)
+    def _(i):
+        at = block(i, piece)
+        wide = resid_ref[at, :].astype(jnp.float32)
+        scale = lax.rsqrt(jnp.mean(wide * wide, axis=-1, keepdims=True) + 1e-05)
+        normed[core, at] = (wide * scale * gain_ref[...]).astype(jnp.bfloat16)
+
+    norm_copy = remote(normed.at[core], normed.at[core], norm_s, norm_r, mate)
+    norm_copy.start()
+    remote(normed.at[core], normed.at[1 - core], norm_s, norm_r, mate).wait_recv()
+    x_passes()
+    x_waits()
+    tile = min(256, half)
+
+    def project(full, r):
+        @pl.loop(0, half // tile)
+        def _(k):
+            value = jnp.dot(normed[r], full[:, block(k, tile)], preferred_element_type=jnp.float32)
+            made[r, :, :, block(k, tile)] = value.astype(jnp.bfloat16).reshape(batch, length, tile)
+
+    def swap(send, recv):
+        return remote(made.at[1 - core], whole.at[:, :, columns(core)], send, recv, mate)
+
+    def swapped(send, recv):
+        return remote(made.at[core], whole.at[:, :, columns(1 - core)], send, recv, mate)
+
+    def zswap(send, recv):
+        return remote(made.at[1 - core], zwhole.at[:, :, columns(core)], send, recv, mate)
+
+    def zswapped(send, recv):
+        return remote(made.at[core], zwhole.at[:, :, columns(1 - core)], send, recv, mate)
+
+    project(full_x, 1 - core)
+    swap(swap_s, swap_r).start()
+    project(full_x, core)
+    whole[:, :, columns(core)] = made[core]
+    last = length - 16
+
+    def tail_of(r):
+        return made.at[r, :, pl.ds(last, 16), :]
+
+    def tail_at(c):
+        return edge.at[:, :, columns(c)]
+
+    onward = {"dp": lax.rem(chip + 1, nd // 2) * 2}
+    across = {"dp": chip * 2 + 1}
+
+    @pl.when(core == 0)
+    def _():
+        remote(tail_of(0), tail_at(core), edge_s.at[0], edge_r.at[core], across).start()
+
+    @pl.when(core == 1)
+    def _():
+        edge[:, :, columns(core)] = made[0, :, pl.ds(last, 16), :]
+
+    @pl.when(chip < nd // 2 - 1)
+    def _():
+        remote(tail_of(1), tail_at(core), edge_s.at[1], edge_r.at[core], onward).start()
+
+    z_waits, z_sends, z_passes = gather_halves(
+        nd, lambda c: in_z_ref.at[:, columns(c)], lambda d: full_z.at[block(d, feats)], feats,
+        z_l, z_s, z_r, zp_s, zp_r,
+    )
+
+    @pl.when(me == 0)
+    def _():
+        edge[...] = jnp.zeros_like(edge)
+
+    swapped(swap_s, swap_r).wait_recv()
+    swap(swap_s, swap_r).wait_send()
+
+    @pl.when(core == 1)
+    def _():
+        remote(tail_of(0), tail_at(0), edge_s.at[0], edge_r.at[0], mate).wait_recv()
+
+    @pl.when((core == 0) & (chip > 0))
+    def _():
+        for c in range(2):
+            remote(tail_of(1), tail_at(c), edge_s.at[1], edge_r.at[c], mate).wait_recv()
+
+    taps = conv_w_ref.shape[0]
+    lane = min(256, chans)
+
+    @pl.loop(0, chans // lane)
+    def _(k):
+        cols = block(k, lane)
+        for b in range(batch):
+            padded[0:8, :] = edge[b, 8:16, cols].astype(jnp.float32)
+            padded[8:, :] = whole[b, :, cols].astype(jnp.float32)
+            total = jnp.zeros((length, lane), jnp.float32) + conv_b_ref[:, cols]
+            for tap in range(taps):
+                first = 8 - (taps - 1) + tap
+                total = total + conv_w_ref[tap : tap + 1, cols] * padded[first : first + length, :]
+            act[b * length : (b + 1) * length, cols] = total / (1.0 + jnp.exp(-total))
+
+    part[...] = jnp.dot(
+        act[...].astype(jnp.bfloat16), low_w_ref[...], preferred_element_type=jnp.float32
+    ).astype(jnp.bfloat16)
+
+    share = rows // nv
     copies = []
     for shift in range(1, nv):
-        target = lax.rem(me + shift, nv)
+        target = lax.rem(vme + shift, nv)
         copy = remote(
-            part_ref.at[pl.ds(pl.multiple_of(target * rows, rows), rows)], recv.at[shift - 1],
-            s1.at[shift - 1], r1.at[shift - 1], peer("vocab", shift),
+            part.at[block(target, share)], low_recv.at[shift - 1],
+            l1_s.at[shift - 1], l1_r.at[shift - 1], peer("vocab", shift),
         )
         copy.start()
         copies.append(copy)
-    own = pl.ds(pl.multiple_of(me * rows, rows), rows)
-    total = part_ref[own, :].astype(jnp.float32)
+    own = block(vme, share)
+    total = part[own, :].astype(jnp.float32)
     for shift in range(1, nv):
         copies[shift - 1].wait()
-        total = total + recv[shift - 1].astype(jnp.float32)
+        total = total + low_recv[shift - 1].astype(jnp.float32)
     dt = total[:, :ranks]
     scale = lax.rsqrt(jnp.mean(dt * dt, axis=-1, keepdims=True) + 1e-06)
-    mine[:, :ranks] = (dt * scale * gain_ref[...]).astype(jnp.bfloat16)
-    mine[:, ranks:] = total[:, ranks:].astype(jnp.bfloat16)
+    low_mine[:, :ranks] = (dt * scale * dt_gain_ref[...]).astype(jnp.bfloat16)
+    low_mine[:, ranks:] = total[:, ranks:].astype(jnp.bfloat16)
     copies = []
     for shift in range(1, nv):
-        copy = remote(
-            mine, out_ref.at[own], s2.at[shift - 1], r2.at[shift - 1], peer("vocab", shift)
-        )
+        copy = remote(low_mine, low.at[own], l2_s.at[shift - 1], l2_r.at[shift - 1], peer("vocab", shift))
         copy.start()
         copies.append(copy)
-    out_ref[own, :] = mine[...]
+    low[own, :] = low_mine[...]
     for copy in copies:
         copy.wait()
 
-
-def dt_reduce(part, gain, nv, ranks):
-    rows, cols = part.shape
-    sems = [pltpu.SemaphoreType.DMA((nv - 1,))] * 4
-    return call(
-        functools.partial(dt_kernel, nv, ranks),
-        jax.ShapeDtypeStruct((rows, cols), jnp.bfloat16),
-        [
-            pltpu.VMEM((nv - 1, rows // nv, cols), jnp.bfloat16),
-            pltpu.VMEM((rows // nv, cols), jnp.bfloat16),
-        ] + sems,
-        1, 10, "dt_reduce",
-    )(part, gain)
-
-
-def scan_kernel(
-    nd, batch, nstate, ranks, low_ref, proj_ref, bias_ref, conv_ref, rate_ref, out_ref,
-    step, drive, maps, result, state, sums, agg, tot, agg_in, tot_in, s1, r1, s2, r2,
-):
-    me = lax.axis_index("dp")
-    rows, chans = conv_ref.shape
     lanes = chans // LANE
-    length = rows // batch
     span = length // CHUNKS
-    greet(("dp",))
-    low_dt = low_ref[:, :ranks]
-    maps[...] = low_ref[:, ranks:].astype(jnp.float32)
+    low_dt = low[:, :ranks]
+    maps[...] = low[:, ranks:].astype(jnp.float32)
     wide = 2 if lanes % 2 == 0 else 1
     size = wide * LANE
 
@@ -120,72 +206,82 @@
             low_dt, proj_ref[:, cols], preferred_element_type=jnp.float32
         ) + bias_ref[:, cols]
         value = jnp.maximum(raw, 0.0) + jnp.log1p(jnp.exp(-jnp.abs(raw)))
-        pushed = value * conv_ref[:, cols]
+        pushed = value * act[:, cols]
         for w in range(wide):
             k = g * wide + w
             step[k] = value[:, w * LANE : (w + 1) * LANE]
             drive[k] = pushed[:, w * LANE : (w + 1) * LANE]
 
-    def run(with_out):
-        @pl.loop(0, lanes // wide)
+    for n in range(2 * nstate):
+        spread[n] = jnp.broadcast_to(maps[:, n : n + 1], (rows, LANE))
+
+    def local_scan(group):
+        @pl.loop(0, lanes // group)
         def _(g):
             for b in range(batch):
                 rates = [
                     [
-                        rate_ref[pl.ds(n, 1), pl.ds(pl.multiple_of((g * wide + w) * LANE, LANE), LANE)]
+                        rate_ref[pl.ds(n, 1), pl.ds(pl.multiple_of((g * group + w) * LANE, LANE), LANE)]
                         for n in range(nstate)
                     ]
-                    for w in range(wide)
+                    for w in range(group)
                 ]
 
                 def one(t, carry):
                     at = pl.ds(b * length + t, CHUNKS, stride=span)
-                    both = maps[at, :]
                     held, extra = carry
                     held, extra = list(held), list(extra)
-                    now = [step[g * wide + w, at, :] for w in range(wide)]
-                    push = [drive[g * wide + w, at, :] for w in range(wide)]
-                    acc = [None] * wide
+                    now = [step[g * group + w, at, :] for w in range(group)]
+                    push = [drive[g * group + w, at, :] for w in range(group)]
                     for n in range(nstate):
-                        into = jnp.broadcast_to(both[:, n : n + 1], (CHUNKS, LANE))
-                        if with_out:
-                            outof = jnp.broadcast_to(
-                                both[:, nstate + n : nstate + n + 1], (CHUNKS, LANE)
-                            )
-                        for w in range(wide):
+                        into = spread[n, at, :]
+                        for w in range(group):
                             i = w * nstate + n
-                            held[i] = (
-                                jnp.exp(-now[w] * rates[w][n]) * held[i] + push[w] * into
-                            )
-                            if with_out:
-                                term = held[i] * outof
-                                acc[w] = term if acc[w] is None else acc[w] + term
-                    for w in range(wide):
-                        if with_out:
-                            result[g * wide + w, at, :] = acc[w]
-                        else:
-                            extra[w] = extra[w] + now[w]
+                            factor = jnp.exp(-now[w] * rates[w][n])
+                            decay[b * span + t, g * group + w, pl.ds(n * CHUNKS, CHUNKS), :] = factor
+                            held[i] = factor * held[i] + push[w] * into
+                    for w in range(group):
+                        extra[w] = extra[w] + now[w]
                     return tuple(held), tuple(extra)
 
                 zero = jnp.zeros((CHUNKS, LANE), jnp.float32)
-                if with_out:
-                    first = tuple(
-                        state[b, g * wide + w, pl.ds(n * CHUNKS, CHUNKS), :]
-                        for w in range(wide) for n in range(nstate)
-                    )
-                    lax.fori_loop(0, span, one, (first, ()))
-                else:
-                    held, extra = lax.fori_loop(
-                        0, span, one, ((zero,) * (wide * nstate), (zero,) * wide)
-                    )
-                    for w in range(wide):
-                        for n in range(nstate):
-                            state[b, g * wide + w, pl.ds(n * CHUNKS, CHUNKS), :] = held[
-                                w * nstate + n
-                            ]
-                        sums[b, g * wide + w] = extra[w]
-
-    run(False)
+                held, extra = lax.fori_loop(0, span, one, ((zero,) * (group * nstate), (zero,) * group))
+                for w in range(group):
+                    for n in range(nstate):
+                        state[b, g * group + w, pl.ds(n * CHUNKS, CHUNKS), :] = held[w * nstate + n]
+                    sums[b, g * group + w] = extra[w]
+
+    def final_scan(group):
+        @pl.loop(0, lanes // group)
+        def _(g):
+            for b in range(batch):
+                def one(t, carry):
+                    at = pl.ds(b * length + t, CHUNKS, stride=span)
+                    held = list(carry)
+                    push = [drive[g * group + w, at, :] for w in range(group)]
+                    acc = [None] * group
+                    for n in range(nstate):
+                        into = spread[n, at, :]
+                        outof = spread[nstate + n, at, :]
+                        for w in range(group):
+                            i = w * nstate + n
+                            factor = decay[b * span + t, g * group + w, pl.ds(n * CHUNKS, CHUNKS), :]
+                            held[i] = factor * held[i] + push[w] * into
+                            term = held[i] * outof
+                            acc[w] = term if acc[w] is None else acc[w] + term
+                    for w in range(group):
+                        result[g * group + w, at, :] = acc[w]
+                    return tuple(held)
+
+                lax.fori_loop(
+                    0, span, one,
+                    tuple(
+                        state[b, g * group + w, pl.ds(n * CHUNKS, CHUNKS), :]
+                        for w in range(group) for n in range(nstate)
+                    ),
+                )
+
+    local_scan(2 if lanes % 2 == 0 else 1)
 
     @pl.loop(0, lanes)
     def _(k):
@@ -236,40 +332,96 @@
                 state[b, k, at, :] = carry
                 carry = jnp.exp(-sums[b, k, pl.ds(c, 1), :] * rate) * carry + part
 
-    run(True)
+    z_passes()
+    final_scan(2 if lanes % 2 == 0 else 1)
+
+    @pl.when(core == 0)
+    def _():
+        remote(tail_of(0), tail_at(core), edge_s.at[0], edge_r.at[core], across).wait_send()
+
+    @pl.when(chip < nd // 2 - 1)
+    def _():
+        remote(tail_of(1), tail_at(core), edge_s.at[1], edge_r.at[core], onward).wait_send()
+
+    z_waits()
+    project(full_z, 1 - core)
+    zswap(zswap_s, zswap_r).start()
+    project(full_z, core)
+    zwhole[:, :, columns(core)] = made[core]
+    zswapped(zswap_s, zswap_r).wait_recv()
 
     @pl.loop(0, lanes)
     def _(k):
-        out_ref[:, pl.ds(pl.multiple_of(k * LANE, LANE), LANE)] = result[k]
+        cols = block(k, LANE)
+        for b in range(batch):
+            gate = zwhole[b, :, cols].astype(jnp.float32)
+            at = pl.ds(b * length, length)
+            gated_ref[at, cols] = (result[k, at] * (gate / (1.0 + jnp.exp(-gate)))).astype(jnp.bfloat16)
 
     for other in range(nd):
         @pl.when(other > me)
         def _():
             for copy in pair(me, other):
                 copy.wait_send()
-
-
-def scan(low, proj, bias, conv, rate, batch, nd, ranks):
-    rows, chans = conv.shape
+    norm_copy.wait_send()
+    zswap(zswap_s, zswap_r).wait_send()
+    x_sends()
+    z_sends()
+
+
+def front(resid, gain, in_x, in_z, conv_w, conv_b, low_w, dt_gain, proj, bias, rate, batch, nv, nd):
+    rows, width = resid.shape
+    chans = in_x.shape[1]
+    half = chans // 2
+    ranks = proj.shape[0]
     nstate = rate.shape[0]
     lanes = chans // LANE
+    length = rows // batch
+    cols = low_w.shape[1]
+    dma = pltpu.SemaphoreType.DMA
     big = pltpu.VMEM((lanes, rows, LANE), jnp.float32)
-    return call(
-        functools.partial(scan_kernel, nd, batch, nstate, ranks),
-        jax.ShapeDtypeStruct((rows, chans), jnp.float32),
-        [
+    slots = 5 if nd == 8 else nd // 2
+    gathers = [dma, dma((slots, 2)), dma((slots, 2)), dma((2, 2)), dma((2, 2))]
+    anywhere = pl.BlockSpec(memory_space=pl.ANY)
+    return pl.pallas_call(
+        functools.partial(front_kernel, nv, nd, batch, ranks, nstate),
+        out_shape=jax.ShapeDtypeStruct((rows, chans), jnp.bfloat16),
+        in_specs=[VMEM, VMEM, anywhere, anywhere] + [VMEM] * 7,
+        out_specs=VMEM,
+        scratch_shapes=[
+            pltpu.VMEM((2, rows, width), jnp.bfloat16),
+            pltpu.VMEM((width, half), jnp.bfloat16),
+            pltpu.VMEM((width, half), jnp.bfloat16),
+            pltpu.VMEM((2, batch, length, half), jnp.bfloat16),
+            pltpu.VMEM((batch, length, chans), jnp.bfloat16),
+            pltpu.VMEM((batch, length, chans), jnp.bfloat16),
+            pltpu.VMEM((batch, 16, chans), jnp.bfloat16),
+            pltpu.VMEM((length + 8, min(256, chans)), jnp.float32),
+            pltpu.VMEM((rows, chans), jnp.float32),
+            pltpu.VMEM((rows, cols), jnp.bfloat16),
+            pltpu.VMEM((nv - 1, rows // nv, cols), jnp.bfloat16),
+            pltpu.VMEM((rows // nv, cols), jnp.bfloat16),
+            pltpu.VMEM((rows, cols), jnp.bfloat16),
             big, big,
-            pltpu.VMEM((rows, low.shape[1] - ranks), jnp.float32),
+            pltpu.VMEM((rows, cols - ranks), jnp.float32),
             big,
+            pltpu.VMEM((rows // CHUNKS, lanes, nstate * CHUNKS, LANE), jnp.float32),
+            pltpu.VMEM((2 * nstate, rows, LANE), jnp.float32),
             pltpu.VMEM((batch, lanes, nstate * CHUNKS, LANE), jnp.float32),
             pltpu.VMEM((batch, lanes, CHUNKS, LANE), jnp.float32),
             pltpu.VMEM((batch * nstate, chans), jnp.bfloat16),
             pltpu.VMEM((batch, chans), jnp.float32),
             pltpu.VMEM((nd, batch * nstate, chans), jnp.bfloat16),
             pltpu.VMEM((nd, batch, chans), jnp.float32),
-        ] + [pltpu.SemaphoreType.DMA((nd,))] * 4,
-        2, 30, "scan",
-    )(low, proj, bias, conv, rate)
+            dma, dma,
+        ] + gathers + gathers + [dma, dma, dma((2,)), dma((2,)), dma, dma]
+        + [dma((nv - 1,))] * 4 + [dma((nd,))] * 4,
+        compiler_params=pltpu.CompilerParams(
+            collective_id=2, has_side_effects=True, vmem_limit_bytes=56 * 1024 * 1024
+        ),
+        cost_estimate=pl.CostEstimate(flops=0, bytes_accessed=int(90 * 3.0e6), transcendentals=0),
+        name="front",
+    )(resid, gain, in_x, in_z, conv_w, conv_b, low_w, dt_gain, proj, bias, rate)
 
 
 def back_kernel(
@@ -698,10 +850,6 @@
     )(gated, w, resid, gain, head, ids, mask)
 
 
-def rms_norm(values, gain, epsilon):
-    return values * lax.rsqrt(jnp.mean(values * values, axis=-1, keepdims=True) + epsilon) * gain
-
-
 def body(
     resid, norm_gain, in_x, in_z, conv_w, conv_b, xdt_w, xbc_w, dt_gain, dt_proj, dt_bias,
     a_rate, out_w, final_gain, head_w, targets, lengths,
@@ -710,43 +858,15 @@
     batch, local_len, width = resid.shape
     channels = in_x.shape[1]
     nstate = a_rate.shape[1]
-    ranks = xdt_w.shape[1]
-    kernel_len = conv_w.shape[0]
     rows = batch * local_len
-
-    full_x = lax.all_gather(in_x, "dp", axis=0, tiled=True)
-    in_z, _ = lax.optimization_barrier((in_z, in_x))
-    full_z = lax.all_gather(in_z, "dp", axis=0, tiled=True)
 
     pad = -(2 * nstate) % 128
     low_w = jnp.concatenate([xdt_w, xbc_w, jnp.zeros((channels, pad), jnp.bfloat16)], axis=1)
     flat = resid.reshape(rows, width)
-    stream = flat.astype(jnp.float32)
-    normed = rms_norm(stream, norm_gain, 1e-05).astype(jnp.bfloat16)
-    x_inner = (
-        jnp.dot(normed, full_x, preferred_element_type=jnp.float32)
-        .astype(jnp.bfloat16)
-        .reshape(batch, local_len, channels)
+    gated = front(
+        flat, norm_gain[None, :], in_x, in_z, conv_w, conv_b[None, :], low_w, dt_gain[None, :], dt_proj,
+        dt_bias[None, :], a_rate.T, batch, nv, nd,
     )
-    before = lax.ppermute(
-        x_inner[:, local_len - (kernel_len - 1) :, :], "dp", [(i, i + 1) for i in range(nd - 1)]
-    )
-    padded = jnp.concatenate([before, x_inner], axis=1).astype(jnp.float32)
-    conv_sum = jnp.zeros((batch, local_len, channels), jnp.float32) + conv_b
-    for tap in range(kernel_len):
-        conv_sum = conv_sum + conv_w[tap] * padded[:, tap : tap + local_len, :]
-    conv_act = jax.nn.silu(conv_sum).reshape(rows, channels)
-    part = jnp.dot(
-        conv_act.astype(jnp.bfloat16), low_w, preferred_element_type=jnp.float32
-    ).astype(jnp.bfloat16)
-    low = dt_reduce(part, dt_gain[None, :], nv, ranks)
-    mixed = scan(low, dt_proj, dt_bias[None, :], conv_act, a_rate.T, batch, nd, ranks)
-    z_gate = (
-        jnp.dot(normed, full_z, preferred_element_type=jnp.float32)
-        .astype(jnp.bfloat16)
-        .astype(jnp.float32)
-    )
-    gated = (mixed * jax.nn.silu(z_gate)).astype(jnp.bfloat16)
     share = width // nv
     positions = lax.axis_index("dp") * local_len + jnp.arange(local_len, dtype=jnp.int32)
     mask = (positions[None, :] < lengths[:, None]).astype(jnp.float32).reshape(1, rows)

time: 260 us -> 203 us (0.78)
  waiting for transfers between devices: 58.4 us -> 0 us
  Pallas kernels: 160 us -> 190 us
  matrix products: 13.9 us -> 0 us
  between operations: 16.7 us -> 3.14 us
    all_gather x2 -> x0, waiting for transfers between devices: 57 us -> none  [the longest x1 57 us: body(): full_x = lax.all_gather(in_x, 'dp', axis=0, tiled=True)]
    pallas_call x2 -> x1, Pallas kernels: 55.6 us -> 94.8 us  [front(): pl.pallas_call(functools.partial(front_kernel, nv, nd, batch, ranks, nsta...]
    dot_general x3 -> x0, matrix products: 13.9 us -> none  [the longest x1 6.94 us: body(): jnp.dot(normed, full_z, preferred_element_type=jnp.float32)]
    pallas_call x1, Pallas kernels: 105 us -> 95.3 us  [back(): pl.pallas_call(functools.partial(back_kernel, nv, nd, steps, relay_at), o...]
  transfers between devices with their start and end apart: 3 -> 0, of which waited for: 1 -> 0; matrix products, arithmetic and copies ran while one was open for 4% -> 0% of each run, Pallas kernels for 21% -> 0%
where the time goes in v2:
time: 203 us
  Pallas kernels  190 us (94%)
  local copies, waits for them, and re-layouts  5.98 us (3%)
  other arithmetic  3.32 us (2%)
  between operations  3.14 us (2%)
    pallas_call x1, Pallas kernels, back(): pl.pallas_call(functools.partial(back_kernel, nv, nd, steps, relay_at), o...  95.3 us
    pallas_call x1, Pallas kernels, front(): pl.pallas_call(functools.partial(front_kernel, nv, nd, batch, ranks, nsta...  94.8 us
    unnamed x7, local copies, waits for them, and re-layouts  4.12 us

profile of v2, /device:TPU:0, one launch (start us, length us, event | category | flops | bytes accessed | tf_op | source)
XLA Modules:
  0.0 202.6 jit_solution(16561013392896847935)
XLA Ops:
  0.6 1.0 copy.20
  1.7 0.1 pad.2.clone
  1.7 2.1 %maximum_maximum_fusion.low_w_ref = bf16[1024,384]{1,0:T(8,128)(2,1)} fusion(bf16[1024,32]{1,0:T(8,128)(2,1)S(1)} %copy.20, bf16[1024,256]{1,0:T(8,128)(2,1)} %param.23, bf16[384]{0:T(512)(128)(2,1)S(1)} %pad.2.clone), kind=kLoop, calls=%fused_computation | loop fusion | flops 2359296 | bytes 1377024 | tf_op jit(solution)/shard_map/concatenate | solution.py:864
  3.8 0.0 copy-start
  3.8 0.0 copy-start.1
  3.8 94.8 %front.1.gated_ref = bf16[256,1024]{1,0:T(8,128)(2,1)} custom-call(bf16[256,4096]{1,0:T(8,128)(2,1)} %bitcast.12, f32[1,4096]{1,0:T(1,128)} %bitcast.16, bf16[512,1024]{1,0:T(8,128)(2,1)} %in_x_ref.1, bf16[512,1024]{1,0:T(8,128)(2,1)} %in_z_ref.1, f32[4,1024]{1,0:T(4,128)} %conv_w_ref.1, f32[1,1024]{1,0:T(1,128)} %bitcast.18, ...), custom_call_target="tpu_custom_call" | custom-call | bytes 270000000 | tf_op jit(solution)/shard_map/front/pallas_call | solution.py:386
  98.6 0.0 copy-done
  98.6 0.6 broadcast_in_dim.34.ids_ref
  99.2 0.0 copy-done.1
  99.2 0.6 compare_convert_fusion
  99.9 95.3 %back.1 = (bf16[256,1024]{1,0:T(8,128)(2,1)}, f32[1,256]{1,0:T(1,128)}, f32[8,128]{1,0:T(8,128)}) custom-call(bf16[256,1024]{1,0:T(8,128)(2,1)} %front.1.gated_ref, bf16[1024,4096]{1,0:T(8,128)(2,1)} %w_ref.1, bf16[256,4096]{1,0:T(8,128)(2,1)} %bitcast.13, f32[1,4096]{1,0:T(1,128)} %bitcast.17, bf16[2048,512]{1,0:T(8,128)(2,1)} %head_ref.1, ...), custom_call_target="tpu_custom_call" | custom-call | bytes 240000000 | tf_op jit(solution)/shard_map/back/pallas_call | solution.py:817
  195.2 1.2 slice.3
  196.4 0.6 convert_reduce_fusion
  198.3 1.9 copy.23
  200.2 1.2 copy.24
  (2 shorter events, 0.0 us)
Async XLA Ops:
  3.8 94.8 %copy-start = (s32[2,128]{1,0:T(2,128)S(1)}, s32[2,128]{1,0:T(2,128)}, u32[]{:S(2)}) copy-start(s32[2,128]{1,0:T(2,128)} %param.32) | copy-start | bytes 3076
  3.8 95.4 %copy-start.1 = (s32[2]{0:T(128)S(1)}, s32[2]{0:T(128)}, u32[]{:S(2)}) copy-start(s32[2]{0:T(128)} %param.33) | copy-start | bytes 28

commit v3 on v2

--- a/solution.py
+++ b/solution.py
@@ -36,7 +36,7 @@
 
 
 def front_kernel(
-    nv, nd, batch, ranks, nstate, resid_ref, gain_ref, in_x_ref, in_z_ref, conv_w_ref, conv_b_ref, low_w_ref,
+    nv, nd, batch, ranks, nstate, resid_ref, gain_ref, in_x_ref, in_z_ref, conv_w_ref, conv_b_ref, xdt_ref, xbc_ref,
     dt_gain_ref, proj_ref, bias_ref, rate_ref, gated_ref,
     normed, full_x, full_z, made, whole, zwhole, edge, padded, act, part, low_recv, low_mine, low,
     step, drive, maps, result, decay, spread, state, sums, agg, tot, agg_in, tot_in,
@@ -160,8 +160,11 @@
                 total = total + conv_w_ref[tap : tap + 1, cols] * padded[first : first + length, :]
             act[b * length : (b + 1) * length, cols] = total / (1.0 + jnp.exp(-total))
 
-    part[...] = jnp.dot(
-        act[...].astype(jnp.bfloat16), low_w_ref[...], preferred_element_type=jnp.float32
+    act_low = act[...].astype(jnp.bfloat16)
+    part[:, ranks:] = jnp.zeros((rows, part.shape[1] - ranks), jnp.bfloat16)
+    part[:, :ranks] = jnp.dot(act_low, xdt_ref[...], preferred_element_type=jnp.float32).astype(jnp.bfloat16)
+    part[:, ranks : ranks + 2 * nstate] = lax.dot_general(
+        act_low, xbc_ref[...], (((1,), (1,)), ((), ())), preferred_element_type=jnp.float32
     ).astype(jnp.bfloat16)
 
     share = rows // nv
@@ -212,8 +215,12 @@
             step[k] = value[:, w * LANE : (w + 1) * LANE]
             drive[k] = pushed[:, w * LANE : (w + 1) * LANE]
 
-    for n in range(2 * nstate):
-        spread[n] = jnp.broadcast_to(maps[:, n : n + 1], (rows, LANE))
+    @pl.loop(0, batch * span)
+    def _(q):
+        b = q // span
+        both = maps[pl.ds(b * length + q - b * span, CHUNKS, stride=span), :]
+        for n in range(2 * nstate):
+            spread[n, block(q, CHUNKS), :] = jnp.broadcast_to(both[:, n : n + 1], (CHUNKS, LANE))
 
     def local_scan(group):
         @pl.loop(0, lanes // group)
@@ -234,7 +241,7 @@
                     now = [step[g * group + w, at, :] for w in range(group)]
                     push = [drive[g * group + w, at, :] for w in range(group)]
                     for n in range(nstate):
-                        into = spread[n, at, :]
+                        into = spread[n, block(b * span + t, CHUNKS), :]
                         for w in range(group):
                             i = w * nstate + n
                             factor = jnp.exp(-now[w] * rates[w][n])
@@ -261,8 +268,8 @@
                     push = [drive[g * group + w, at, :] for w in range(group)]
                     acc = [None] * group
                     for n in range(nstate):
-                        into = spread[n, at, :]
-                        outof = spread[nstate + n, at, :]
+                        into = spread[n, block(b * span + t, CHUNKS), :]
+                        outof = spread[nstate + n, block(b * span + t, CHUNKS), :]
                         for w in range(group):
                             i = w * nstate + n
                             factor = decay[b * span + t, g * group + w, pl.ds(n * CHUNKS, CHUNKS), :]
@@ -369,7 +376,7 @@
     z_sends()
 
 
-def front(resid, gain, in_x, in_z, conv_w, conv_b, low_w, dt_gain, proj, bias, rate, batch, nv, nd):
+def front(resid, gain, in_x, in_z, conv_w, conv_b, xdt, xbc, dt_gain, proj, bias, rate, batch, nv, nd):
     rows, width = resid.shape
     chans = in_x.shape[1]
     half = chans // 2
@@ -377,7 +384,7 @@
     nstate = rate.shape[0]
     lanes = chans // LANE
     length = rows // batch
-    cols = low_w.shape[1]
+    cols = ranks + 2 * nstate + -(ranks + 2 * nstate) % LANE
     dma = pltpu.SemaphoreType.DMA
     big = pltpu.VMEM((lanes, rows, LANE), jnp.float32)
     slots = 5 if nd == 8 else nd // 2
@@ -386,7 +393,7 @@
     return pl.pallas_call(
         functools.partial(front_kernel, nv, nd, batch, ranks, nstate),
         out_shape=jax.ShapeDtypeStruct((rows, chans), jnp.bfloat16),
-        in_specs=[VMEM, VMEM, anywhere, anywhere] + [VMEM] * 7,
+        in_specs=[VMEM, VMEM, anywhere, anywhere] + [VMEM] * 8,
         out_specs=VMEM,
         scratch_shapes=[
             pltpu.VMEM((2, rows, width), jnp.bfloat16),
@@ -421,11 +428,11 @@
         ),
         cost_estimate=pl.CostEstimate(flops=0, bytes_accessed=int(90 * 3.0e6), transcendentals=0),
         name="front",
-    )(resid, gain, in_x, in_z, conv_w, conv_b, low_w, dt_gain, proj, bias, rate)
+    )(resid, gain, in_x, in_z, conv_w, conv_b, xdt, xbc, dt_gain, proj, bias, rate)
 
 
 def back_kernel(
-    nv, nd, steps, relay_at, gated_ref, w_ref, resid_ref, gain_ref, head_ref, ids_ref, mask_ref,
+    nv, nd, steps, relay_at, gated_ref, w_ref, resid_ref, gain_ref, head_ref, ids_ref, lengths_ref,
     hidden_ref, logp_ref, sum_ref,
     weight, own, near, send_up, recv_up, send_down, recv_down, hid, fin, full, logits, ids, stats, heard,
     part, parts, w_sem, near_sem, up_s, up_r, down_s, down_r, gup_s, gup_r, gdown_s, gdown_r,
@@ -437,6 +444,7 @@
     mate = {"dp": chip * 2 + 1 - core}
     above, below = {"vocab": lax.rem(me + 1, nv)}, {"vocab": lax.rem(me + nv - 1, nv)}
     rows, chans = gated_ref.shape
+    batch, length = ids_ref.shape
     width = w_ref.shape[1]
     share = width // nv
     entries, feats = head_ref.shape
@@ -625,7 +633,7 @@
             )
 
         top = lax.fori_loop(0, half // vt, highest, jnp.full((1, rows), -jnp.inf, jnp.float32))
-        wanted = ids[s, 0:1, :] - (me * entries + core * half)
+        wanted = jnp.concatenate([ids[s, b : b + 1, :] for b in range(batch)], axis=1) - (me * entries + core * half)
 
         def gather(k, carry):
             total, picked = carry
@@ -670,8 +678,14 @@
         total = total + one[1:2] * jnp.exp(one[0:1] - top)
         picked = picked + one[2:3]
     logp = picked - (top + jnp.log(total))
-    logp_ref[...] = logp
-    masked = jnp.sum(jnp.where(mask_ref[...] > 0.0, logp, 0.0), axis=-1, keepdims=True)
+    place = lax.broadcasted_iota(jnp.int32, (1, length), 1) + dev * length
+    masked = jnp.zeros((1, 1), jnp.float32)
+    count = jnp.zeros((1, 1), jnp.float32)
+    for b in range(batch):
+        part_logp = logp[:, b * length : (b + 1) * length]
+        logp_ref[b : b + 1, :] = part_logp
+        masked = masked + jnp.sum(jnp.where(place < lengths_ref[b], part_logp, 0.0), axis=-1, keepdims=True)
+        count = count + lengths_ref[b].astype(jnp.float32)
     part[...] = jnp.broadcast_to(masked, part.shape)
     for shift in range(1, nd):
         copy = remote(
@@ -687,7 +701,7 @@
     grand = parts[0]
     for d in range(1, nd):
         grand = grand + parts[d]
-    sum_ref[...] = grand
+    sum_ref[...] = grand[0:1, 0:1] / count
 
     for copy in sends:
         copy.wait_send()
@@ -804,7 +818,7 @@
     return finish_waits, finish_sends, passes
 
 
-def back(gated, w, resid, gain, head, ids, mask, nv, nd, steps=4, relay_at=3):
+def back(gated, w, resid, gain, head, ids, lengths, nv, nd, steps=4, relay_at=3):
     rows, chans = gated.shape
     width = w.shape[1]
     share = width // nv
@@ -818,10 +832,10 @@
         functools.partial(back_kernel, nv, nd, steps, relay_at),
         out_shape=(
             jax.ShapeDtypeStruct((rows, share), jnp.bfloat16),
-            jax.ShapeDtypeStruct((1, rows), jnp.float32),
-            jax.ShapeDtypeStruct((8, LANE), jnp.float32),
+            jax.ShapeDtypeStruct(ids.shape, jnp.float32),
+            jax.ShapeDtypeStruct((1, 1), jnp.float32),
         ),
-        in_specs=[VMEM, anywhere, anywhere, VMEM, anywhere, VMEM, VMEM],
+        in_specs=[VMEM, anywhere, anywhere, VMEM, anywhere, VMEM, pl.BlockSpec(memory_space=pltpu.SMEM)],
         out_specs=(VMEM, VMEM, VMEM),
         scratch_shapes=[
             pltpu.VMEM((chans, width), jnp.bfloat16),
@@ -832,7 +846,7 @@
             pltpu.VMEM((2, rows, width), jnp.bfloat16),
             pltpu.VMEM((half, width), jnp.bfloat16),
             pltpu.VMEM((half, 2 * rows), jnp.float32),
-            pltpu.VMEM((2, 8, rows), jnp.int32),
+            pltpu.VMEM((2,) + ids.shape, jnp.int32),
             pltpu.VMEM((2, 8, rows), jnp.float32),
             pltpu.VMEM((nv, 2, 8, rows), jnp.float32),
             pltpu.VMEM((8, LANE), jnp.float32),
@@ -847,7 +861,7 @@
         ),
         cost_estimate=pl.CostEstimate(flops=0, bytes_accessed=int(80 * 3.0e6), transcendentals=0),
         name="back",
-    )(gated, w, resid, gain, head, ids, mask)
+    )(gated, w, resid, gain, head, ids, lengths)
 
 
 def body(
@@ -857,26 +871,21 @@
     nv, nd = lax.axis_size("vocab"), lax.axis_size("dp")
     batch, local_len, width = resid.shape
     channels = in_x.shape[1]
-    nstate = a_rate.shape[1]
     rows = batch * local_len
 
-    pad = -(2 * nstate) % 128
-    low_w = jnp.concatenate([xdt_w, xbc_w, jnp.zeros((channels, pad), jnp.bfloat16)], axis=1)
     flat = resid.reshape(rows, width)
     gated = front(
-        flat, norm_gain[None, :], in_x, in_z, conv_w, conv_b[None, :], low_w, dt_gain[None, :], dt_proj,
+        flat, norm_gain[None, :], in_x, in_z, conv_w, conv_b[None, :], xdt_w, xbc_w.T, dt_gain[None, :], dt_proj,
         dt_bias[None, :], a_rate.T, batch, nv, nd,
     )
     share = width // nv
-    positions = lax.axis_index("dp") * local_len + jnp.arange(local_len, dtype=jnp.int32)
-    mask = (positions[None, :] < lengths[:, None]).astype(jnp.float32).reshape(1, rows)
-    ids = jnp.broadcast_to(targets.reshape(1, rows), (8, rows))
-    hidden_share, logp, grand = back(gated, out_w, flat, final_gain[None, :], head_w, ids, mask, nv, nd)
-    mean_logp = grand[0, 0] / jnp.sum(lengths.astype(jnp.float32))
+    hidden_share, logp, mean_logp = back(
+        gated, out_w, flat, final_gain[None, :], head_w, targets, lengths, nv, nd
+    )
     return (
         hidden_share.reshape(batch, local_len, share),
-        logp.reshape(batch, local_len),
-        mean_logp,
+        logp,
+        mean_logp.reshape(()),
     )
 
 

time: 203 us -> 196 us (0.966)
  other arithmetic: 3.32 us -> 0 us
  local copies, waits for them, and re-layouts: 5.98 us -> 3.11 us
    concatenate x1 -> x0, other arithmetic: 2.09 us -> none  [body(): jnp.concatenate([xdt_w, xbc_w, jnp.zeros((channels, pad), jnp.bfloat16)],...]
    unnamed x7 -> x2, local copies, waits for them, and re-layouts: 4.12 us -> 3.11 us
where the time goes in v3:
time: 196 us; the launch traced here: 195 us
  Pallas kernels  190 us (97%)
  local copies, waits for them, and re-layouts  3.11 us (2%)
  between operations  2.41 us (1%)
    pallas_call x1, Pallas kernels, front(): pl.pallas_call(functools.partial(front_kernel, nv, nd, batch, ranks, nsta...  95.8 us
    pallas_call x1, Pallas kernels, back(): pl.pallas_call(functools.partial(back_kernel, nv, nd, steps, relay_at), o...  94.2 us

profile of v3, /device:TPU:0, one launch (start us, length us, event | category | flops | bytes accessed | tf_op | source)
XLA Modules:
  0.0 195.5 jit_solution(945354899107332224)
XLA Ops:
  0.6 95.8 %front.1.gated_ref = bf16[256,1024]{1,0:T(8,128)(2,1)} custom-call(bf16[256,4096]{1,0:T(8,128)(2,1)} %bitcast.10, f32[1,4096]{1,0:T(1,128)} %bitcast.15, bf16[512,1024]{1,0:T(8,128)(2,1)} %in_x_ref.1, bf16[512,1024]{1,0:T(8,128)(2,1)} %in_z_ref.1, f32[4,1024]{1,0:T(4,128)} %conv_w_ref.1, f32[1,1024]{1,0:T(1,128)} %bitcast.17, bf16[1024,256]{1,0:T(8,128)(2,1)} %xdt_ref.1, ...), custom_call_target="tpu_custom_call" | custom-call | bytes 270000000 | tf_op jit(solution)/shard_map/front/pallas_call | solution.py:393
  96.4 94.2 %back.1 = (bf16[256,1024]{1,0:T(8,128)(2,1)}, f32[2,128]{1,0:T(2,128)}, f32[1,1]{1,0:T(1,128)}) custom-call(bf16[256,1024]{1,0:T(8,128)(2,1)} %front.1.gated_ref, bf16[1024,4096]{1,0:T(8,128)(2,1)} %w_ref.1, bf16[256,4096]{1,0:T(8,128)(2,1)} %bitcast.11, f32[1,4096]{1,0:T(1,128)} %bitcast.16, bf16[2048,512]{1,0:T(8,128)(2,1)} %head_ref.1, s32[2,128]{1,0:T(2,128)} %ids_ref.1, ...), custom_call_target="tpu_custom_call" | custom-call | bytes 240000000 | tf_op jit(solution)/shard_map/back/pallas_call | solution.py:831
  190.6 1.9 copy.23
  192.5 1.2 copy.24

commit v4 on v3

--- a/solution.py
+++ b/solution.py
@@ -315,6 +315,7 @@
             for copy in pair(me, other):
                 copy.start()
 
+    z_passes()
     for other in range(nd):
         @pl.when(other < me)
         def _():
@@ -339,7 +340,6 @@
                 state[b, k, at, :] = carry
                 carry = jnp.exp(-sums[b, k, pl.ds(c, 1), :] * rate) * carry + part
 
-    z_passes()
     final_scan(2 if lanes % 2 == 0 else 1)
 
     @pl.when(core == 0)

time: 196 us -> 192 us (0.980)
  Pallas kernels: 190 us -> 187 us
    pallas_call x1, Pallas kernels: 95.8 us -> 90.9 us  [front(): pl.pallas_call(functools.partial(front_kernel, nv, nd, batch, ranks, nsta...]
where the time goes in v4:
time: 192 us
  Pallas kernels  187 us (97%)
  local copies, waits for them, and re-layouts  3.11 us (2%)
  between operations  2.41 us (1%)
    pallas_call x1, Pallas kernels, back(): pl.pallas_call(functools.partial(back_kernel, nv, nd, steps, relay_at), o...  95.8 us
    pallas_call x1, Pallas kernels, front(): pl.pallas_call(functools.partial(front_kernel, nv, nd, batch, ranks, nsta...  90.9 us

profile of v4, /device:TPU:0, one launch (start us, length us, event | category | flops | bytes accessed | tf_op | source)
XLA Modules:
  0.0 192.2 jit_solution(15005040233296478625)
XLA Ops:
  0.6 90.9 %front.1.gated_ref = bf16[256,1024]{1,0:T(8,128)(2,1)} custom-call(bf16[256,4096]{1,0:T(8,128)(2,1)} %bitcast.10, f32[1,4096]{1,0:T(1,128)} %bitcast.15, bf16[512,1024]{1,0:T(8,128)(2,1)} %in_x_ref.1, bf16[512,1024]{1,0:T(8,128)(2,1)} %in_z_ref.1, f32[4,1024]{1,0:T(4,128)} %conv_w_ref.1, f32[1,1024]{1,0:T(1,128)} %bitcast.17, bf16[1024,256]{1,0:T(8,128)(2,1)} %xdt_ref.1, ...), custom_call_target="tpu_custom_call" | custom-call | bytes 270000000 | tf_op jit(solution)/shard_map/front/pallas_call | solution.py:393
  91.5 95.8 %back.1 = (bf16[256,1024]{1,0:T(8,128)(2,1)}, f32[2,128]{1,0:T(2,128)}, f32[1,1]{1,0:T(1,128)}) custom-call(bf16[256,1024]{1,0:T(8,128)(2,1)} %front.1.gated_ref, bf16[1024,4096]{1,0:T(8,128)(2,1)} %w_ref.1, bf16[256,4096]{1,0:T(8,128)(2,1)} %bitcast.11, f32[1,4096]{1,0:T(1,128)} %bitcast.16, bf16[2048,512]{1,0:T(8,128)(2,1)} %head_ref.1, s32[2,128]{1,0:T(2,128)} %ids_ref.1, ...), custom_call_target="tpu_custom_call" | custom-call | bytes 240000000 | tf_op jit(solution)/shard_map/back/pallas_call | solution.py:831
  187.4 1.9 copy.23
  189.2 1.2 copy.24
